TPU v7x, 32 devices: a whole 2x2x4 slice. The times are simulated.
32 devices in a mesh: genome: 8 (over z, x), anc: 4 (over y, core), trait: 1.
Axes of the slice: x: 2, y: 2, z: 4, core: 2. Of those that a mesh axis runs over, the one named last changes fastest.
Arguments:
- coefficients: float32 [4, 128, 16384], P('anc', 'trait', 'genome'), may hold values from -3 to 3
- sumstats: float32 [4, 128, 16384], P('anc', 'trait', 'genome'), may hold values from -12 to 12
- linkage: bfloat16 [4, 16384, 4096], P('anc', 'genome'), may hold values from -0.09375 to 0.09375
- band_start: int32 [4, 64], P('anc', 'genome'), may hold values from 0 to 12288, as said below
- group_ids: int32 [4, 16384], P('anc', 'genome'), may hold values from 0 to 15, never falling along the last dimension, each value on 1 to 8192 neighbouring positions
- group_weight: float32 [4, 16], P('anc'), may hold values from 0.1 to 1.5
- dosage: bfloat16 [4, 2048, 16384], P('anc', None, 'genome'), may hold values from 0 to 2
Outputs:
- updated: float32 [4, 128, 16384], P('anc', 'trait', 'genome')
- scores: float32 [4, 128, 2048], P('anc', 'trait', 'genome')
Inputs may be any that keep to these rules, and one draw needn't show every extreme that they name: band_start[a, u] is the first of the 4096 consecutive SNP columns stored in linkage[a] for row block u, the SNPs u * 256 to u * 256 + 255; these columns always include the block's own SNPs. `group_ids`: group ids never fall along the SNPs of an ancestry, so each group is one run of consecutive SNPs.
All inputs are finite; a program needn't handle non-finite values.
Results may differ from a plain program's by a relative error of at most 0.003.
Values may be sent and summed in bfloat16 or wider, within the bound.
A program may use at most 128 MiB of HBM per device.

v0:
```python
import functools
import math

import jax
import jax.numpy as jnp
from jax import lax
from jax.experimental import pallas as pl
from jax.experimental.pallas import tpu as pltpu
from jax.sharding import PartitionSpec as P

step_size = 0.5
merging = 0.5
epsilon = 1e-06

MESH = pl.DeviceIdType.MESH
F32 = jnp.float32
BF16 = jnp.bfloat16


def step_kernel(
    sizes,
    coef_hbm, sums_hbm, link_hbm, starts_hbm, ids_hbm, weight_hbm, dosage_hbm,
    updated_hbm, score_ref,
    coef, sums, link, starts_ref, ids_ref, weight_ref, dosage, low, ext, extf, peers, proposal, updated, updated_t, row,
    stats_out, stats_in, side_out, side_in, part_out, part_in,
    load_sem, link_sem, store_sem,
    halo_send, halo_recv, anc_send, anc_recv, stats_send, stats_recv, side_send, side_recv, part_send, part_recv,
):
    genomes, ancs, traits_n, reach, tile, groups = sizes
    traits_here, snps = coef.shape
    width = link.shape[1]
    tiles = snps // tile
    persons_per = part_out.shape[1]
    g = lax.axis_index("genome")
    a = lax.axis_index("anc")
    t = lax.axis_index("trait")
    stat_peers = [(k, m) for m in range(traits_n) for k in range(genomes) if (k, m) != (0, 0)]

    def genome_peer(k):
        return lax.rem(g + k, genomes)

    load_coef = pltpu.make_async_copy(coef_hbm.at[0], coef, load_sem.at[0])
    load_coef.start()
    barrier = pltpu.get_barrier_semaphore()
    for k, m in stat_peers:
        pl.semaphore_signal(
            barrier, inc=1, device_id_type=MESH,
            device_id={"genome": genome_peer(k), "trait": lax.rem(t + m, traits_n)},
        )
    for k in range(1, ancs):
        pl.semaphore_signal(
            barrier, inc=1, device_id={"anc": lax.rem(a + k, ancs)}, device_id_type=MESH
        )
    load_sums = pltpu.make_async_copy(sums_hbm.at[0], sums, load_sem.at[1])
    load_sums.start()
    load_small = [
        pltpu.make_async_copy(starts_hbm, starts_ref, load_sem.at[3]),
        pltpu.make_async_copy(ids_hbm, ids_ref, load_sem.at[4]),
        pltpu.make_async_copy(weight_hbm, weight_ref, load_sem.at[5]),
    ]
    for load in load_small:
        load.start()
    load_dosage = pltpu.make_async_copy(dosage_hbm.at[0], dosage, load_sem.at[2])

    def link_copy(u):
        rows = pl.ds(pl.multiple_of(u * tile, tile), tile)
        return pltpu.make_async_copy(link_hbm.at[0, rows, :], link.at[rows, :], link_sem.at[u])

    load_coef.wait()

    half = snps // 2
    even = 1 - 2 * lax.rem(g, 2)
    near, far, across = g + even, g + 2 * even, g - even

    def in_range(p):
        return jnp.logical_and(p >= 0, p < genomes)

    def own_block(u, carry):
        cols = pl.ds(pl.multiple_of(u * tile, tile), tile)
        block = coef[:, cols].astype(BF16)
        low[:, cols] = block
        flat = block.astype(F32).T
        extf[pl.ds(pl.multiple_of(reach * snps + u * tile, tile), tile), :] = flat
        ext[reach, cols, :] = flat.astype(BF16)
        return carry

    def halo_copy(src_slot, dst_slot, h, peer, send):
        rows = pl.ds(h * half, half)
        return pltpu.make_async_remote_copy(
            src_ref=ext.at[src_slot, rows, :], dst_ref=ext.at[dst_slot, rows, :],
            send_sem=halo_send.at[send], recv_sem=halo_recv.at[dst_slot, h],
            device_id={"genome": jnp.clip(peer, 0, genomes - 1)}, device_id_type=MESH,
        )

    def near_copy(h):
        return halo_copy(reach, reach - even, h, near, h)

    def far_copy(d, h):
        return halo_copy(reach, reach - d, h, g + d, (2 if d > 0 else 4) + h)

    def relay_far():
        return halo_copy(reach + even, reach - even, 0, far, 6)

    def relay_near():
        return halo_copy(reach + 2 * even, reach + even, 1, near, 7)

    def arrived(slot, h):
        halo_copy(reach, slot, h, near, 0).wait_recv()

    def anc_copy(k):
        return pltpu.make_async_remote_copy(
            src_ref=low, dst_ref=peers.at[k - 1],
            send_sem=anc_send.at[k - 1], recv_sem=anc_recv.at[k - 1],
            device_id={"anc": lax.rem(a + k, ancs)}, device_id_type=MESH,
        )

    def far_each(h):
        for d in (2, -2):
            @pl.when(in_range(g + d))
            def _(d=d):
                far_copy(d, h).start()

    lax.fori_loop(0, tiles // 2, own_block, 0, unroll=2)
    pl.semaphore_wait(barrier, len(stat_peers) + ancs - 1)
    near_copy(0).start()
    lax.fori_loop(tiles // 2, tiles, own_block, 0, unroll=2)
    far_each(1)
    near_copy(1).start()
    far_each(0)
    for k in range(1, ancs):
        anc_copy(k).start()
    for u in range(tiles):
        link_copy(u).start()
    load_dosage.start()

    chunk = 256

    def widen(slot, h):
        def piece(i, carry):
            at = pl.multiple_of(h * half + i * chunk, chunk)
            extf[pl.ds(pl.multiple_of(slot * snps + at, chunk), chunk), :] = (
                ext[slot, pl.ds(at, chunk), :].astype(F32)
            )
            return carry

        lax.fori_loop(0, half // chunk, piece, 0, unroll=2)

    for d in (-2, -1, 1, 2):
        @pl.when(jnp.logical_not(in_range(g + d)))
        def _(slot=reach + d):
            def clear(i, carry):
                at = pl.multiple_of(slot * snps + i * chunk, chunk)
                extf[pl.ds(at, chunk), :] = jnp.zeros((chunk, traits_here), F32)
                return carry

            lax.fori_loop(0, snps // chunk, clear, 0)

    arrived(reach + even, 0)

    @pl.when(in_range(far))
    def _():
        relay_far().start()
        arrived(reach + 2 * even, 1)
        relay_near().start()

    widen(reach + even, 0)

    @pl.when(in_range(far))
    def _():
        widen(reach + 2 * even, 1)

    @pl.when(in_range(g - 2 * even))
    def _():
        arrived(reach - 2 * even, 1)
        widen(reach - 2 * even, 1)

    arrived(reach + even, 1)
    widen(reach + even, 1)

    @pl.when(in_range(far))
    def _():
        arrived(reach + 2 * even, 0)
        widen(reach + 2 * even, 0)

    @pl.when(in_range(g - 2 * even))
    def _():
        arrived(reach - 2 * even, 0)
        widen(reach - 2 * even, 0)

    @pl.when(in_range(across))
    def _():
        for h in range(2):
            arrived(reach - even, h)
            widen(reach - even, h)

    load_sums.wait()
    for load in load_small:
        load.wait()

    def band_tile(u, carry):
        link_copy(u).wait()
        rows = pl.ds(pl.multiple_of(u * tile, tile), tile)
        begin = jnp.clip(starts_ref[0, u] - g * snps + reach * snps, 0, extf.shape[0] - width)
        depth = 512
        total = jnp.zeros((tile, traits_here), F32)
        for c in range(0, width, depth):
            window = extf[pl.ds(begin + c, depth), :].astype(BF16)
            total = total + jnp.dot(
                link[rows, c:c + depth], window, preferred_element_type=F32
            )
        band = total.T
        current = coef[:, rows]
        proposal[:, rows] = current + band - sums[:, rows]
        return carry

    lax.fori_loop(0, tiles, band_tile, 0, unroll=2)
    for k in range(1, ancs):
        anc_copy(k).wait_recv()

    def propose(u, carry):
        cols = pl.ds(pl.multiple_of(u * tile, tile), tile)
        current = coef[:, cols]
        mean = current
        for k in range(1, ancs):
            mean = mean + peers[k - 1, :, cols].astype(F32)
        mean = mean / ancs
        gradient = proposal[:, cols] + merging * (current - mean)
        value = current - step_size * gradient
        proposal[:, cols] = value
        row[:, cols] = jnp.sum(value * value, axis=0, keepdims=True)
        return carry

    lax.fori_loop(0, tiles, propose, 0, unroll=2)

    group_of = lax.broadcasted_iota(jnp.int32, (groups, snps), 0)
    mine = group_of == ids_ref[...]
    squares = jnp.sum(jnp.where(mine, row[...], 0.0), axis=1, keepdims=True)
    counts = jnp.sum(jnp.where(mine, 1.0, 0.0), axis=1, keepdims=True)
    lane = lax.broadcasted_iota(jnp.int32, (groups, 128), 1)
    stats = jnp.where(lane == 0, squares, jnp.where(lane == 1, counts, 0.0))
    stats_out[...] = stats

    def stats_copy(i):
        k, m = stat_peers[i]
        return pltpu.make_async_remote_copy(
            src_ref=stats_out, dst_ref=stats_in.at[i],
            send_sem=stats_send.at[i], recv_sem=stats_recv.at[i],
            device_id={"genome": genome_peer(k), "trait": lax.rem(t + m, traits_n)},
            device_id_type=MESH,
        )

    for i in range(len(stat_peers)):
        stats_copy(i).start()
    load_dosage.wait()
    for i in range(len(stat_peers)):
        stats_copy(i).wait_recv()
        stats = stats + stats_in[i]
    all_squares = stats[:, 0:1]
    all_counts = stats[:, 1:2] / traits_n
    square_of = lax.broadcasted_iota(jnp.int32, (groups, groups), 0)
    lane_of = lax.broadcasted_iota(jnp.int32, (groups, groups), 1)
    weight = jnp.sum(
        jnp.where(square_of == lane_of, weight_ref[...], 0.0), axis=1, keepdims=True
    )
    threshold = step_size * weight * jnp.sqrt(all_counts * (traits_here * traits_n))
    shrink = jnp.maximum(0.0, 1.0 - threshold / jnp.sqrt(all_squares + epsilon))
    row[...] = jnp.sum(jnp.where(mine, shrink, 0.0), axis=0, keepdims=True)

    def shrink_tile(u, carry):
        cols = pl.ds(pl.multiple_of(u * tile, tile), tile)
        value = proposal[:, cols] * row[:, cols]
        updated[:, cols] = value
        updated_t[cols, :] = value.T.astype(BF16)
        return carry

    lax.fori_loop(0, tiles, shrink_tile, 0, unroll=2)
    store = pltpu.make_async_copy(updated, updated_hbm.at[0], store_sem)
    store.start()

    scale = 1.0 / math.sqrt(snps * genomes)

    pairs = genomes // 2
    own_side, other_side = lax.rem(g, 2), lax.rem(near, 2)

    def pair_at(i):
        k = pairs // 2 + (1 - 2 * lax.rem(i, 2)) * ((i + 1) // 2)
        return lax.rem(g // 2 + k + pairs, pairs)

    def partial(person):
        at = pl.ds(pl.multiple_of(person * persons_per, persons_per), persons_per)
        return jnp.dot(dosage[at, :], updated_t[...], preferred_element_type=F32) * scale

    def side_copy(i):
        return pltpu.make_async_remote_copy(
            src_ref=side_out.at[i], dst_ref=side_in.at[i],
            send_sem=side_send.at[i], recv_sem=side_recv.at[i],
            device_id={"genome": near}, device_id_type=MESH,
        )

    def part_copy(i):
        return pltpu.make_async_remote_copy(
            src_ref=part_out.at[i], dst_ref=part_in.at[i],
            send_sem=part_send.at[i], recv_sem=part_recv.at[i],
            device_id={"genome": 2 * pair_at(i) + own_side}, device_id_type=MESH,
        )

    def send_side(i, carry):
        side_out[i] = partial(2 * pair_at(i) + other_side).astype(BF16)
        side_copy(i).start()
        return carry

    def pair_sum(i):
        mine_here = partial(2 * pair_at(i) + own_side)
        side_copy(i).wait_recv()
        return mine_here + side_in[i].astype(F32)

    def send_part(i, carry):
        part_out[i] = pair_sum(i).astype(BF16)
        part_copy(i).start()
        return carry

    lax.fori_loop(0, pairs, send_side, 0)
    lax.fori_loop(0, pairs - 1, send_part, 0)

    def add_part(i, total):
        part_copy(i).wait_recv()
        return total + part_in[i].astype(F32)

    score_ref[0] = lax.fori_loop(0, pairs - 1, add_part, pair_sum(pairs - 1)).T

    store.wait()
    for h in range(2):
        near_copy(h).wait_send()
        for d in (2, -2):
            @pl.when(in_range(g + d))
            def _(d=d, h=h):
                far_copy(d, h).wait_send()

    @pl.when(in_range(far))
    def _():
        relay_far().wait_send()
        relay_near().wait_send()

    for k in range(1, ancs):
        anc_copy(k).wait_send()
    for i in range(len(stat_peers)):
        stats_copy(i).wait_send()

    def sent_side(i, carry):
        side_copy(i).wait_send()
        return carry

    def sent_part(i, carry):
        part_copy(i).wait_send()
        return carry

    lax.fori_loop(0, pairs, sent_side, 0)
    lax.fori_loop(0, pairs - 1, sent_part, 0)


def per_device(coefficients, sumstats, linkage, band_start, group_ids, group_weight, dosage):
    _, traits_here, snps = coefficients.shape
    width = linkage.shape[2]
    genomes = lax.axis_size("genome")
    ancs = lax.axis_size("anc")
    traits_n = lax.axis_size("trait")
    persons = dosage.shape[1]
    persons_per = persons // genomes
    groups = group_weight.shape[1]
    reach = -(-width // snps)
    assert reach == 2 and genomes % 2 == 0 and coefficients.shape[0] == 1
    tile = snps // band_start.shape[1]
    slots = 2 * reach + 1
    pairs = genomes // 2
    stat_n = genomes * traits_n - 1
    sizes = (genomes, ancs, traits_n, reach, tile, groups)
    anyspace = pl.BlockSpec(memory_space=pl.ANY)
    hbm = pl.BlockSpec(memory_space=pltpu.HBM)
    vmem = pl.BlockSpec(memory_space=pltpu.VMEM)
    dma = pltpu.SemaphoreType.DMA
    return pl.pallas_call(
        functools.partial(step_kernel, sizes),
        out_shape=(
            jax.ShapeDtypeStruct((1, traits_here, snps), F32),
            jax.ShapeDtypeStruct((1, traits_here, persons_per), F32),
        ),
        in_specs=[hbm] * 7,
        out_specs=(anyspace, vmem),
        scratch_shapes=[
            pltpu.VMEM((traits_here, snps), F32),
            pltpu.VMEM((traits_here, snps), F32),
            pltpu.VMEM((snps, width), BF16),
            pltpu.SMEM(band_start.shape, jnp.int32),
            pltpu.VMEM(group_ids.shape, jnp.int32),
            pltpu.VMEM(group_weight.shape, F32),
            pltpu.VMEM((persons, snps), BF16),
            pltpu.VMEM((traits_here, snps), BF16),
            pltpu.VMEM((slots, snps, traits_here), BF16),
            pltpu.VMEM((slots * snps, traits_here), F32),
            pltpu.VMEM((ancs - 1, traits_here, snps), BF16),
            pltpu.VMEM((traits_here, snps), F32),
            pltpu.VMEM((traits_here, snps), F32),
            pltpu.VMEM((snps, traits_here), BF16),
            pltpu.VMEM((1, snps), F32),
            pltpu.VMEM((groups, 128), F32),
            pltpu.VMEM((stat_n, groups, 128), F32),
            pltpu.VMEM((pairs, persons_per, traits_here), BF16),
            pltpu.VMEM((pairs, persons_per, traits_here), BF16),
            pltpu.VMEM((pairs - 1, persons_per, traits_here), BF16),
            pltpu.VMEM((pairs - 1, persons_per, traits_here), BF16),
            dma((6,)), dma((snps // tile,)), dma,
            dma((8,)), dma((slots, 2)), dma((ancs - 1,)), dma((ancs - 1,)),
            dma((stat_n,)), dma((stat_n,)), dma((pairs,)), dma((pairs,)), dma((pairs - 1,)), dma((pairs - 1,)),
        ],
        compiler_params=pltpu.CompilerParams(
            collective_id=0, has_side_effects=True, vmem_limit_bytes=52 * 1024 * 1024
        ),
    )(coefficients, sumstats, linkage, band_start, group_ids, group_weight, dosage)


def solution(mesh):
    in_specs = (
        P("anc", "trait", "genome"),
        P("anc", "trait", "genome"),
        P("anc", "genome", None),
        P("anc", "genome"),
        P("anc", "genome"),
        P("anc", None),
        P("anc", None, "genome"),
    )
    out_specs = (P("anc", "trait", "genome"), P("anc", "trait", "genome"))
    return jax.shard_map(
        per_device, mesh=mesh, in_specs=in_specs, out_specs=out_specs, check_vma=False
    )
```

profile of v0, /device:TPU:0, one launch (start us, length us, event | category | flops | bytes accessed | tf_op | source)
XLA Modules:
  0.0 51.4 jit_solution(15492033870777654878)
XLA Ops:
  0.6 0.0 copy-start
  0.6 0.7 %copy-done = s32[1,2048]{1,0:T(1,128)S(1)} copy-done((s32[1,2048]{1,0:T(1,128)S(1)}, s32[1,2048]{1,0:T(1,128)}, u32[]{:S(2)}) %copy-start) | copy-done | bytes 8216
  1.3 0.0 copy-start.1
  1.3 0.7 %copy-done.1 = s32[1,8]{1,0:T(1,128)S(1)} copy-done((s32[1,8]{1,0:T(1,128)S(1)}, s32[1,8]{1,0:T(1,128)}, u32[]{:S(2)}) %copy-start.1) | copy-done | bytes 56
  2.0 0.0 copy-start.2
  2.0 0.7 %copy-done.2 = f32[1,16]{1,0:T(1,128)S(1)} copy-done((f32[1,16]{1,0:T(1,128)S(1)}, f32[1,16]{1,0:T(1,128)}, u32[]{:S(2)}) %copy-start.2) | copy-done | bytes 88
  2.6 47.1 %shard_map.86 = (f32[1,128,2048]{2,1,0:T(8,128)S(1)}, f32[1,128,256]{2,1,0:T(8,128)S(1)}) custom-call(f32[1,128,2048]{2,1,0:T(8,128)} %coef_hbm.1, f32[1,128,2048]{2,1,0:T(8,128)} %sums_hbm.1, bf16[1,2048,4096]{2,1,0:T(8,128)(2,1)} %link_hbm.1, s32[1,8]{1,0:T(1,128)S(1)} %copy-done.1, s32[1,2048]{1,0:T(1,128)S(1)} %copy-done, f32[1,16]{1,0:T(1,128)S(1)} %copy-done.2, ...), custom_call_target="tpu_custom_call" | custom-call | tf_op jit(solution)/shard_map/pallas_call | solution.py:381
  49.8 1.0 %copy.11 = f32[1,128,2048]{2,1,0:T(8,128)} copy(f32[1,128,2048]{2,1,0:T(8,128)S(1)} %get-tuple-element.4) | data formatting | bytes 2097152
  50.7 0.7 %copy.12 = f32[1,128,256]{2,1,0:T(8,128)} copy(f32[1,128,256]{2,1,0:T(8,128)S(1)} %get-tuple-element.5) | data formatting | bytes 262144
Async XLA Ops:
  0.6 0.7 %copy-start = (s32[1,2048]{1,0:T(1,128)S(1)}, s32[1,2048]{1,0:T(1,128)}, u32[]{:S(2)}) copy-start(s32[1,2048]{1,0:T(1,128)} %ids_hbm.1) | copy-start | bytes 24580
  1.3 0.7 %copy-start.1 = (s32[1,8]{1,0:T(1,128)S(1)}, s32[1,8]{1,0:T(1,128)}, u32[]{:S(2)}) copy-start(s32[1,8]{1,0:T(1,128)} %starts_hbm.1) | copy-start | bytes 100
  2.0 0.7 %copy-start.2 = (f32[1,16]{1,0:T(1,128)S(1)}, f32[1,16]{1,0:T(1,128)}, u32[]{:S(2)}) copy-start(f32[1,16]{1,0:T(1,128)} %weight_hbm.1) | copy-start | bytes 196
where the time goes:
time: 51.6 us; the launch traced here: 51.4 us
  Pallas kernels  47.1 us (91%)
  local copies, waits for them, and re-layouts  3.63 us (7%)
  between operations  0.65 us (1%)
    pallas_call x1, Pallas kernels, per_device(): pl.pallas_call(functools.partial(step_kernel, sizes), out_shape=(jax.Shap...  47.1 us
    unnamed x8, local copies, waits for them, and re-layouts  3.63 us

commit v1 on v0

v1 whole, which is shorter than its diff:
```python
import functools
import math

import jax
import jax.numpy as jnp
from jax import lax
from jax.experimental import pallas as pl
from jax.experimental.pallas import tpu as pltpu
from jax.sharding import PartitionSpec as P

step_size = 0.5
merging = 0.5
epsilon = 1e-06
longest_run = 8192

MESH = pl.DeviceIdType.MESH
F32 = jnp.float32
BF16 = jnp.bfloat16


def step_kernel(
    sizes,
    coef_hbm, sums_hbm, link_hbm, starts_hbm, ids_hbm, weight_hbm, dosage_hbm,
    updated_ref, score_ref,
    coef, sums, link, starts_ref, ids_ref, weight_ref, dosage, ext, extf, pair, mean, pair_out, pair_in,
    proposal, low, row, stats_out, stats_in, side_out, side_in, part_out, part_in,
    coef_sem, load_sem, link_sem, ready,
    halo_send, halo_recv, pair_send, pair_recv, stats_send, stats_recv, side_send, side_recv, part_send, part_recv,
):
    genomes, ancs, traits_n, reach, tile, groups = sizes
    traits_here, snps = coef.shape
    width = link.shape[1]
    tiles = snps // tile
    persons_per = part_out.shape[2]
    pairs = genomes // 2
    g = lax.axis_index("genome")
    a = lax.axis_index("anc")
    t = lax.axis_index("trait")
    core, side = lax.rem(a, 2), a // 2
    parity = lax.rem(g, 2)
    even = 1 - 2 * parity
    near, far, back, across = g + even, g + 2 * even, g - 2 * even, g - even

    def in_range(p):
        return jnp.logical_and(p >= 0, p < genomes)

    def genome(p):
        return {"genome": jnp.clip(p, 0, genomes - 1)}

    group_reach = min(-(-longest_run // snps), genomes - 1)
    stat_peers = [
        (d, m) for m in range(traits_n) for d in range(-group_reach, group_reach + 1) if (d, m) != (0, 0)
    ]
    if genomes > 8 or traits_n > 1:
        greet = [(k, m) for m in range(traits_n) for k in range(genomes) if (k, m) != (0, 0)]
    else:
        greet = []

    coef_parts = coef_sem.shape[0]
    part_cols = snps // coef_parts

    def coef_copy(i):
        cols = pl.ds(i * part_cols, part_cols)
        return pltpu.make_async_copy(coef_hbm.at[0, :, cols], coef.at[:, cols], coef_sem.at[i])

    for i in range(coef_parts):
        coef_copy(i).start()
    barrier = pltpu.get_barrier_semaphore()
    if greet:
        for k, m in greet:
            pl.semaphore_signal(
                barrier, inc=1, device_id_type=MESH,
                device_id={"genome": lax.rem(g + k, genomes), "trait": lax.rem(t + m, traits_n)},
            )
        expected = len(greet)
    else:
        pl.semaphore_signal(barrier, inc=1, device_id=genome(near), device_id_type=MESH)
        for peer in (far, back):
            @pl.when(in_range(peer))
            def _(peer=peer):
                pl.semaphore_signal(barrier, inc=1, device_id=genome(peer), device_id_type=MESH)
        expected = 1 + in_range(far).astype(jnp.int32) + in_range(back).astype(jnp.int32)

    @pl.when(core == 0)
    def _():
        pl.semaphore_signal(barrier, inc=1, device_id={"anc": a + 1}, device_id_type=MESH)

    @pl.when(jnp.logical_and(core == 1, side == 1))
    def _():
        pl.semaphore_signal(barrier, inc=1, device_id={"anc": a - 2}, device_id_type=MESH)

    expected = expected + core + core * (1 - side)

    load_small = [
        pltpu.make_async_copy(starts_hbm, starts_ref, load_sem.at[0]),
        pltpu.make_async_copy(ids_hbm, ids_ref, load_sem.at[1]),
        pltpu.make_async_copy(weight_hbm, weight_ref, load_sem.at[2]),
    ]
    load_sums = pltpu.make_async_copy(sums_hbm.at[0], sums, load_sem.at[3])
    load_dosage = pltpu.make_async_copy(dosage_hbm.at[0], dosage, load_sem.at[4])

    def link_copy(u):
        rows = pl.ds(pl.multiple_of(u * tile, tile), tile)
        return pltpu.make_async_copy(link_hbm.at[0, rows, :], link.at[rows, :], link_sem.at[u])

    def own_block(u, carry):
        cols = pl.ds(pl.multiple_of(u * tile, tile), tile)
        flat = coef[:, cols].T.astype(BF16)
        ext[reach, cols, :] = flat
        extf[pl.ds(pl.multiple_of(reach * snps + u * tile, tile), tile), :] = flat.astype(F32)
        return carry

    for i in range(coef_parts):
        coef_copy(i).wait()
        lax.fori_loop(i * tiles // coef_parts, (i + 1) * tiles // coef_parts, own_block, 0, unroll=2)

    unit = snps // 16
    far_rows = width - tile - snps
    f_rows, n_rows = 9 * unit, 7 * unit
    rest = far_rows - n_rows
    half_far = far_rows // 2

    def piece(p, odd):
        f_base, n_base = (1 - odd) * n_rows, odd * f_rows
        if p < 3:
            at, size = f_base + p * 3 * unit, 3 * unit
        elif p == 3:
            at, size = n_base, 4 * unit
        elif p == 4:
            at, size = n_base + 4 * unit, 3 * unit
        elif p == 5:
            at, size = (1 - odd) * n_rows + odd * (snps - far_rows), rest
        else:
            at, size = (1 - odd) * (snps - far_rows) + (p - 6) * half_far, half_far
        return pl.multiple_of(at, unit), size

    def halo_copy(src_slot, dst_slot, p, odd, peer, send):
        at, size = piece(p, odd)
        rows = pl.ds(at, size)
        return pltpu.make_async_remote_copy(
            src_ref=ext.at[src_slot, rows, :], dst_ref=ext.at[dst_slot, rows, :],
            send_sem=halo_send.at[send], recv_sem=halo_recv.at[dst_slot, p],
            device_id=genome(peer), device_id_type=MESH,
        )

    def near_copy(p):
        return halo_copy(reach, reach - even, p, parity, near, p)

    def back_copy(p):
        return halo_copy(reach, reach + 2 * even, p, parity, back, 5 + p - 3)

    def far_copy(p):
        return halo_copy(reach, reach - 2 * even, p, parity, far, 8 + p - 6)

    def relay_far(p):
        return halo_copy(reach + even, reach - even, p, 1 - parity, far, 10 + p)

    def relay_near(p):
        return halo_copy(reach + 2 * even, reach + even, p, parity, near, 13 + p - 3)

    def arrived(slot, p, odd):
        halo_copy(reach, slot, p, odd, near, 0).wait_recv()

    has_far, has_back = in_range(far), in_range(back)

    pl.semaphore_wait(barrier, expected)

    def start_back(p):
        @pl.when(has_back)
        def _():
            back_copy(p).start()

    def start_far(p):
        @pl.when(has_far)
        def _():
            far_copy(p).start()

    near_copy(0).start()
    start_back(3)
    start_far(6)
    near_copy(1).start()
    start_back(4)
    start_far(7)
    near_copy(2).start()
    start_back(5)
    near_copy(3).start()
    near_copy(4).start()

    @pl.when(core == 1)
    def _():
        pl.semaphore_signal(ready, inc=1, device_id={"anc": a - 1}, device_id_type=MESH)

    @pl.when(jnp.logical_and(core == 1, side == 0))
    def _():
        pl.semaphore_signal(ready, inc=1, device_id={"anc": a + 2}, device_id_type=MESH)

    for load in load_small:
        load.start()
    load_sums.start()
    for u in range(tiles):
        link_copy(u).start()
    load_dosage.start()

    other_core = {"anc": a + 1 - 2 * core}
    other_side = {"anc": lax.rem(a + 2, ancs)}
    up_copy = pltpu.make_async_remote_copy(
        src_ref=coef, dst_ref=pair, send_sem=pair_send.at[0], recv_sem=pair_recv.at[0],
        device_id=other_core, device_id_type=MESH,
    )
    over_copy = pltpu.make_async_remote_copy(
        src_ref=pair_out, dst_ref=pair_in, send_sem=pair_send.at[1], recv_sem=pair_recv.at[1],
        device_id=other_side, device_id_type=MESH,
    )
    down_copy = pltpu.make_async_remote_copy(
        src_ref=mean, dst_ref=mean, send_sem=pair_send.at[2], recv_sem=pair_recv.at[2],
        device_id=other_core, device_id_type=MESH,
    )

    chunk = unit

    def widen(slot, p, odd):
        at, size = piece(p, odd)

        def part(i, carry):
            r = pl.multiple_of(at + i * chunk, chunk)
            extf[pl.ds(pl.multiple_of(slot * snps + r, chunk), chunk), :] = ext[slot, pl.ds(r, chunk), :].astype(F32)
            return carry

        lax.fori_loop(0, size // chunk, part, 0)

    def clear(slot):
        def part(i, carry):
            at = pl.multiple_of(slot * snps + i * chunk, chunk)
            extf[pl.ds(at, chunk), :] = jnp.zeros((chunk, traits_here), F32)
            return carry

        lax.fori_loop(0, snps // chunk, part, 0)

    for d in (-1, 1):
        @pl.when(jnp.logical_not(in_range(g + d)))
        def _(d=d):
            clear(reach + d)

    clear(0)
    clear(2 * reach)

    for i, (d, m) in enumerate(stat_peers):
        @pl.when(jnp.logical_not(in_range(g - d)))
        def _(i=i):
            stats_in[i] = jnp.zeros(stats_in.shape[1:], F32)

    def pass_on(p):
        if p < 3:
            arrived(reach + even, p, 1 - parity)

            @pl.when(has_far)
            def _():
                relay_far(p).start()
        else:
            @pl.when(has_far)
            def _():
                arrived(reach + 2 * even, p, parity)
                relay_near(p).start()

    pass_on(0)
    pass_on(3)

    @pl.when(core == 0)
    def _():
        pl.semaphore_wait(ready, 1)
        up_copy.start()

    pass_on(1)
    pass_on(4)

    @pl.when(core == 1)
    def _():
        up_copy.wait_recv()

        def add(u, carry):
            cols = pl.ds(pl.multiple_of(u * tile, tile), tile)
            value = coef[:, cols] + pair[:, cols]
            pair[:, cols] = value
            pair_out[:, cols] = value.astype(BF16)
            return carry

        lax.fori_loop(0, tiles, add, 0)

        @pl.when(side == 1)
        def _():
            pl.semaphore_wait(ready, 1)

        over_copy.start()

    pass_on(2)
    for p in range(3):
        widen(reach + even, p, 1 - parity)

    @pl.when(has_far)
    def _():
        arrived(reach + 2 * even, 5, parity)
        for p in (3, 4, 5):
            widen(reach + 2 * even, p, parity)

    for p in (3, 4):
        arrived(reach + even, p, 1 - parity)
        widen(reach + even, p, 1 - parity)

    @pl.when(has_back)
    def _():
        for p in (6, 7):
            arrived(reach - 2 * even, p, parity)
            widen(reach - 2 * even, p, parity)

    @pl.when(core == 1)
    def _():
        over_copy.wait_recv()

        def add(u, carry):
            cols = pl.ds(pl.multiple_of(u * tile, tile), tile)
            mean[:, cols] = (pair[:, cols] + pair_in[:, cols].astype(F32)) / ancs
            return carry

        lax.fori_loop(0, tiles, add, 0)
        down_copy.start()

    @pl.when(core == 0)
    def _():
        down_copy.wait_recv()

    load_sums.wait()
    for load in load_small:
        load.wait()

    def prepare(u, carry):
        cols = pl.ds(pl.multiple_of(u * tile, tile), tile)
        proposal[:, cols] = (
            (1.0 - step_size - step_size * merging) * coef[:, cols]
            + step_size * sums[:, cols] + (step_size * merging) * mean[:, cols]
        )
        return carry

    lax.fori_loop(0, tiles, prepare, 0)

    @pl.when(has_back)
    def _():
        for p in range(5):
            arrived(reach - even, p, 1 - parity)
            widen(reach - even, p, 1 - parity)

    def band_tile(u, carry):
        link_copy(u).wait()
        rows = pl.ds(pl.multiple_of(u * tile, tile), tile)
        begin = jnp.clip(starts_ref[0, u] - g * snps + reach * snps, 0, extf.shape[0] - width)
        depth = 512
        total = jnp.zeros((tile, traits_here), F32)
        for c in range(0, width, depth):
            window = extf[pl.ds(begin + c, depth), :].astype(BF16)
            total = total + jnp.dot(
                link[rows, c:c + depth], window, preferred_element_type=F32
            )
        value = proposal[:, rows] - step_size * total.T
        proposal[:, rows] = value
        row[:, rows] = jnp.sum(value * value, axis=0, keepdims=True)
        return carry

    lax.fori_loop(0, tiles, band_tile, 0, unroll=2)

    lanes = stats_out.shape[1]
    mine = lax.broadcasted_iota(jnp.int32, (groups, snps), 0) == ids_ref[...]
    squares = jnp.sum(jnp.where(mine, row[...], 0.0), axis=1, keepdims=True)
    counts = jnp.sum(jnp.where(mine, 1.0, 0.0), axis=1, keepdims=True)
    on_lane = lax.broadcasted_iota(jnp.int32, (groups, lanes), 0) == lax.broadcasted_iota(
        jnp.int32, (groups, lanes), 1
    )
    stats_out[0:1, :] = jnp.sum(jnp.where(on_lane, squares, 0.0), axis=0, keepdims=True)
    stats_out[1:2, :] = jnp.sum(jnp.where(on_lane, counts, 0.0), axis=0, keepdims=True)

    def stats_copy(i):
        d, m = stat_peers[i]
        return pltpu.make_async_remote_copy(
            src_ref=stats_out, dst_ref=stats_in.at[i],
            send_sem=stats_send.at[i], recv_sem=stats_recv.at[i],
            device_id={**genome(g + d), "trait": lax.rem(t + m, traits_n)}, device_id_type=MESH,
        )

    for i, (d, m) in enumerate(stat_peers):
        @pl.when(in_range(g + d))
        def _(i=i):
            stats_copy(i).start()

    load_dosage.wait()
    for i, (d, m) in enumerate(stat_peers):
        @pl.when(in_range(g - d))
        def _(i=i):
            stats_copy(i).wait_recv()

    stats = stats_out[...]
    for i in range(len(stat_peers)):
        stats = stats + stats_in[i]
    all_squares = stats[0:1, :groups]
    all_counts = stats[1:2, :groups] / traits_n
    threshold = step_size * weight_ref[...] * jnp.sqrt(all_counts * (traits_here * traits_n))
    shrink = jnp.maximum(0.0, 1.0 - threshold / jnp.sqrt(all_squares + epsilon))
    same = lax.broadcasted_iota(jnp.int32, (groups, groups), 0) == lax.broadcasted_iota(
        jnp.int32, (groups, groups), 1
    )
    shrink = jnp.sum(jnp.where(same, shrink, 0.0), axis=1, keepdims=True)
    row[...] = jnp.sum(jnp.where(mine, shrink, 0.0), axis=0, keepdims=True)

    def shrink_tile(u, carry):
        cols = pl.ds(pl.multiple_of(u * tile, tile), tile)
        value = proposal[:, cols] * row[:, cols]
        updated_ref[0, :, cols] = value
        low[:, cols] = value.astype(BF16)
        return carry

    lax.fori_loop(0, tiles, shrink_tile, 0, unroll=2)

    scale = 1.0 / math.sqrt(snps * genomes)
    own_side, other_side_g = parity, lax.rem(near, 2)

    def pair_at(i):
        k = pairs // 2 + (1 - 2 * lax.rem(i, 2)) * ((i + 1) // 2)
        return lax.rem(g // 2 + k + pairs, pairs)

    def partial(person):
        at = pl.ds(pl.multiple_of(person * persons_per, persons_per), persons_per)
        return lax.dot_general(
            low[...], dosage[at, :], (((1,), (1,)), ((), ())), preferred_element_type=F32
        ) * scale

    def side_copy(i):
        return pltpu.make_async_remote_copy(
            src_ref=side_out.at[i], dst_ref=side_in.at[i],
            send_sem=side_send.at[i], recv_sem=side_recv.at[i],
            device_id={"genome": near}, device_id_type=MESH,
        )

    def part_copy(i):
        return pltpu.make_async_remote_copy(
            src_ref=part_out.at[i], dst_ref=part_in.at[i],
            send_sem=part_send.at[i], recv_sem=part_recv.at[i],
            device_id={"genome": 2 * pair_at(i) + own_side}, device_id_type=MESH,
        )

    def send_side(i, carry):
        side_out[i] = partial(2 * pair_at(i) + other_side_g).astype(BF16)
        side_copy(i).start()
        return carry

    def pair_sum(i):
        mine_here = partial(2 * pair_at(i) + own_side)
        side_copy(i).wait_recv()
        return mine_here + side_in[i].astype(F32)

    def send_part(i, carry):
        part_out[i] = pair_sum(i).astype(BF16)
        part_copy(i).start()
        return carry

    lax.fori_loop(0, pairs, send_side, 0)
    lax.fori_loop(0, pairs - 1, send_part, 0)

    def add_part(i, total):
        part_copy(i).wait_recv()
        return total + part_in[i].astype(F32)

    score_ref[0] = lax.fori_loop(0, pairs - 1, add_part, pair_sum(pairs - 1))

    for p in range(5):
        near_copy(p).wait_send()

    @pl.when(has_back)
    def _():
        for p in (3, 4, 5):
            back_copy(p).wait_send()

    @pl.when(has_far)
    def _():
        for p in (6, 7):
            far_copy(p).wait_send()
        for p in (0, 1, 2):
            relay_far(p).wait_send()
        for p in (3, 4):
            relay_near(p).wait_send()

    @pl.when(core == 0)
    def _():
        up_copy.wait_send()

    @pl.when(core == 1)
    def _():
        over_copy.wait_send()
        down_copy.wait_send()

    for i, (d, m) in enumerate(stat_peers):
        @pl.when(in_range(g + d))
        def _(i=i):
            stats_copy(i).wait_send()

    def sent_side(i, carry):
        side_copy(i).wait_send()
        return carry

    def sent_part(i, carry):
        part_copy(i).wait_send()
        return carry

    lax.fori_loop(0, pairs, sent_side, 0)
    lax.fori_loop(0, pairs - 1, sent_part, 0)


def store_kernel(updated_in, score_in, updated_out, score_out, sem):
    copies = [
        pltpu.make_async_copy(updated_in, updated_out, sem.at[0]),
        pltpu.make_async_copy(score_in, score_out, sem.at[1]),
    ]
    for copy in copies:
        copy.start()
    for copy in copies:
        copy.wait()


def per_device(coefficients, sumstats, linkage, band_start, group_ids, group_weight, dosage):
    _, traits_here, snps = coefficients.shape
    width = linkage.shape[2]
    genomes = lax.axis_size("genome")
    ancs = lax.axis_size("anc")
    traits_n = lax.axis_size("trait")
    persons = dosage.shape[1]
    persons_per = persons // genomes
    groups = group_weight.shape[1]
    reach = -(-width // snps)
    assert reach == 2 and genomes % 2 == 0 and coefficients.shape[0] == 1 and ancs == 4
    tile = snps // band_start.shape[1]
    slots = 2 * reach + 1
    pairs = genomes // 2
    group_reach = min(-(-longest_run // snps), genomes - 1)
    stat_n = (2 * group_reach + 1) * traits_n - 1
    lanes = -(-groups // 128) * 128
    sizes = (genomes, ancs, traits_n, reach, tile, groups)
    hbm = pl.BlockSpec(memory_space=pltpu.HBM)
    vmem = pl.BlockSpec(memory_space=pltpu.VMEM)
    dma = pltpu.SemaphoreType.DMA
    args = (coefficients, sumstats, linkage, band_start, group_ids, group_weight, dosage)
    args = tuple(pltpu.with_memory_space_constraint(x, pltpu.HBM) for x in args)
    out_shape = (
        jax.ShapeDtypeStruct((1, traits_here, snps), F32),
        jax.ShapeDtypeStruct((1, traits_here, persons_per), F32),
    )
    updated, scores = pl.pallas_call(
        functools.partial(step_kernel, sizes),
        out_shape=out_shape,
        in_specs=[hbm] * 7,
        out_specs=(vmem, vmem),
        scratch_shapes=[
            pltpu.VMEM((traits_here, snps), F32),
            pltpu.VMEM((traits_here, snps), F32),
            pltpu.VMEM((snps, width), BF16),
            pltpu.SMEM(band_start.shape, jnp.int32),
            pltpu.VMEM(group_ids.shape, jnp.int32),
            pltpu.VMEM(group_weight.shape, F32),
            pltpu.VMEM((persons, snps), BF16),
            pltpu.VMEM((slots, snps, traits_here), BF16),
            pltpu.VMEM((slots * snps, traits_here), F32),
            pltpu.VMEM((traits_here, snps), F32),
            pltpu.VMEM((traits_here, snps), F32),
            pltpu.VMEM((traits_here, snps), BF16),
            pltpu.VMEM((traits_here, snps), BF16),
            pltpu.VMEM((traits_here, snps), F32),
            pltpu.VMEM((traits_here, snps), BF16),
            pltpu.VMEM((1, snps), F32),
            pltpu.VMEM((2, lanes), F32),
            pltpu.VMEM((stat_n, 2, lanes), F32),
            pltpu.VMEM((pairs, traits_here, persons_per), BF16),
            pltpu.VMEM((pairs, traits_here, persons_per), BF16),
            pltpu.VMEM((pairs - 1, traits_here, persons_per), BF16),
            pltpu.VMEM((pairs - 1, traits_here, persons_per), BF16),
            dma((4,)), dma((5,)), dma((snps // tile,)), pltpu.SemaphoreType.REGULAR,
            dma((15,)), dma((slots, 8)), dma((3,)), dma((3,)),
            dma((stat_n,)), dma((stat_n,)), dma((pairs,)), dma((pairs,)), dma((pairs - 1,)), dma((pairs - 1,)),
        ],
        compiler_params=pltpu.CompilerParams(
            collective_id=0, has_side_effects=True, vmem_limit_bytes=52 * 1024 * 1024
        ),
    )(*args)
    return pl.pallas_call(
        store_kernel,
        out_shape=out_shape,
        in_specs=[vmem, vmem],
        out_specs=(hbm, hbm),
        scratch_shapes=[dma((2,))],
    )(*(pltpu.with_memory_space_constraint(x, pltpu.VMEM) for x in (updated, scores)))


def solution(mesh):
    in_specs = (
        P("anc", "trait", "genome"),
        P("anc", "trait", "genome"),
        P("anc", "genome", None),
        P("anc", "genome"),
        P("anc", "genome"),
        P("anc", None),
        P("anc", None, "genome"),
    )
    out_specs = (P("anc", "trait", "genome"), P("anc", "trait", "genome"))
    return jax.shard_map(
        per_device, mesh=mesh, in_specs=in_specs, out_specs=out_specs, check_vma=False
    )
```

time: 51.6 us -> 45.8 us (0.89)
  local copies, waits for them, and re-layouts: 3.63 us -> 0 us
  Pallas kernels: 47.1 us -> 45 us
    unnamed x8 -> x0, local copies, waits for them, and re-layouts: 3.63 us -> none
    pallas_call x1 -> x2, Pallas kernels: 47.1 us -> 45 us  [the longest x1 44 us: per_device(): pl.pallas_call(functools.partial(step_kernel, sizes), out_shape=out_shape...]
where the time goes in v1:
time: 45.8 us; the launch traced here: 45.6 us
  Pallas kernels  45 us (98%)
  between operations  0.64 us (1%)
    pallas_call x1, Pallas kernels, per_device(): pl.pallas_call(functools.partial(step_kernel, sizes), out_shape=out_shape...  44 us
    pallas_call x1, Pallas kernels, per_device(): pl.pallas_call(store_kernel, out_shape=out_shape, in_specs=[vmem, vmem],...  1.02 us

profile of v1, /device:TPU:0, one launch (start us, length us, event | category | flops | bytes accessed | tf_op | source)
XLA Modules:
  0.0 45.6 jit_solution(7034709195557796431)
XLA Ops:
  0.6 44.0 %shard_map.86 = (f32[1,128,2048]{2,1,0:T(8,128)S(1)}, f32[1,128,256]{2,1,0:T(8,128)S(1)}) custom-call(f32[1,128,2048]{2,1,0:T(8,128)} %coef_hbm.1, f32[1,128,2048]{2,1,0:T(8,128)} %sums_hbm.1, bf16[1,2048,4096]{2,1,0:T(8,128)(2,1)} %link_hbm.1, s32[1,8]{1,0:T(1,128)} %starts_hbm.1, s32[1,2048]{1,0:T(1,128)} %ids_hbm.1, f32[1,16]{1,0:T(1,128)} %weight_hbm.1, ...), custom_call_target="tpu_custom_call" | custom-call | tf_op jit(solution)/shard_map/pallas_call | solution.py:552
  44.6 1.0 %shard_map.87 = (f32[1,128,2048]{2,1,0:T(8,128)}, f32[1,128,256]{2,1,0:T(8,128)}) custom-call(f32[1,128,2048]{2,1,0:T(8,128)S(1)} %get-tuple-element.4.updated_in, f32[1,128,256]{2,1,0:T(8,128)S(1)} %get-tuple-element.5.score_in), custom_call_target="tpu_custom_call" | custom-call | tf_op jit(solution)/shard_map/pallas_call | solution.py:588

commit v2 on v1

--- a/solution.py
+++ b/solution.py
@@ -22,15 +22,17 @@
     sizes,
     coef_hbm, sums_hbm, link_hbm, starts_hbm, ids_hbm, weight_hbm, dosage_hbm,
     updated_ref, score_ref,
-    coef, sums, link, starts_ref, ids_ref, weight_ref, dosage, ext, extf, pair, mean, pair_out, pair_in,
+    coef, sums, link_first, link_second, starts_ref, ids_ref, weight_ref, dosage, ext, field, band, pair, mean, pair_out, pair_in,
     proposal, low, row, stats_out, stats_in, side_out, side_in, part_out, part_in,
     coef_sem, load_sem, link_sem, ready,
     halo_send, halo_recv, pair_send, pair_recv, stats_send, stats_recv, side_send, side_recv, part_send, part_recv,
 ):
     genomes, ancs, traits_n, reach, tile, groups = sizes
     traits_here, snps = coef.shape
-    width = link.shape[1]
+    links = (link_first, link_second)
+    width = link_first.shape[1]
     tiles = snps // tile
+    half = tiles // 2
     persons_per = part_out.shape[2]
     pairs = genomes // 2
     g = lax.axis_index("genome")
@@ -100,39 +102,45 @@
     load_dosage = pltpu.make_async_copy(dosage_hbm.at[0], dosage, load_sem.at[4])
 
     def link_copy(u):
-        rows = pl.ds(pl.multiple_of(u * tile, tile), tile)
-        return pltpu.make_async_copy(link_hbm.at[0, rows, :], link.at[rows, :], link_sem.at[u])
+        return pltpu.make_async_copy(
+            link_hbm.at[0, pl.ds(u * tile, tile), :], links[u // half].at[pl.ds(u % half * tile, tile), :],
+            link_sem.at[u],
+        )
+
+    unit = snps // 16
+    far_rows = width - tile - snps
+    ahead = 11 * unit
+    behind = snps - ahead
+    deep = [r + 128 for r in (snps, ahead, behind)]
+    own_at = deep[0]
+    partner_at = own_at + snps + deep[0]
+    back_at = partner_at + snps + deep[0]
+    across_a = back_at + snps + deep[0]
+    far_a = across_a + ahead + deep[1]
+    across_b = far_a + ahead + deep[1]
+    far_b = across_b + behind + deep[2]
+    assert far_b + behind + deep[2] == field.shape[0] and 13 * unit < far_rows <= 16 * unit
 
     def own_block(u, carry):
         cols = pl.ds(pl.multiple_of(u * tile, tile), tile)
         flat = coef[:, cols].T.astype(BF16)
         ext[reach, cols, :] = flat
-        extf[pl.ds(pl.multiple_of(reach * snps + u * tile, tile), tile), :] = flat.astype(F32)
+        field[pl.ds(pl.multiple_of(own_at + u * tile, unit), tile), :] = flat.astype(F32)
         return carry
 
     for i in range(coef_parts):
         coef_copy(i).wait()
         lax.fori_loop(i * tiles // coef_parts, (i + 1) * tiles // coef_parts, own_block, 0, unroll=2)
 
-    unit = snps // 16
-    far_rows = width - tile - snps
-    f_rows, n_rows = 9 * unit, 7 * unit
-    rest = far_rows - n_rows
-    half_far = far_rows // 2
+    pieces = [
+        (5 * unit, 6 * unit), (13 * unit, 3 * unit), (0, 5 * unit), (11 * unit, 2 * unit),
+        (5 * unit, 6 * unit), (13 * unit, far_rows - 13 * unit),
+        (snps - far_rows, far_rows // 2), (snps - far_rows + far_rows // 2, far_rows // 2),
+    ]
 
     def piece(p, odd):
-        f_base, n_base = (1 - odd) * n_rows, odd * f_rows
-        if p < 3:
-            at, size = f_base + p * 3 * unit, 3 * unit
-        elif p == 3:
-            at, size = n_base, 4 * unit
-        elif p == 4:
-            at, size = n_base + 4 * unit, 3 * unit
-        elif p == 5:
-            at, size = (1 - odd) * n_rows + odd * (snps - far_rows), rest
-        else:
-            at, size = (1 - odd) * (snps - far_rows) + (p - 6) * half_far, half_far
-        return pl.multiple_of(at, unit), size
+        at, size = pieces[p]
+        return pl.multiple_of((1 - odd) * at + odd * (snps - at - size), unit), size
 
     def halo_copy(src_slot, dst_slot, p, odd, peer, send):
         at, size = piece(p, odd)
@@ -147,7 +155,7 @@
         return halo_copy(reach, reach - even, p, parity, near, p)
 
     def back_copy(p):
-        return halo_copy(reach, reach + 2 * even, p, parity, back, 5 + p - 3)
+        return halo_copy(reach, reach + 2 * even, p, parity, back, 4 + p - 2)
 
     def far_copy(p):
         return halo_copy(reach, reach - 2 * even, p, parity, far, 8 + p - 6)
@@ -156,7 +164,7 @@
         return halo_copy(reach + even, reach - even, p, 1 - parity, far, 10 + p)
 
     def relay_near(p):
-        return halo_copy(reach + 2 * even, reach + even, p, parity, near, 13 + p - 3)
+        return halo_copy(reach + 2 * even, reach + even, p, parity, near, 12 + p - 2)
 
     def arrived(slot, p, odd):
         halo_copy(reach, slot, p, odd, near, 0).wait_recv()
@@ -165,26 +173,17 @@
 
     pl.semaphore_wait(barrier, expected)
 
-    def start_back(p):
+    for p, q in ((0, 2), (1, 3), (2, 4), (3, 5)):
+        near_copy(p).start()
+
         @pl.when(has_back)
-        def _():
-            back_copy(p).start()
-
-    def start_far(p):
-        @pl.when(has_far)
-        def _():
-            far_copy(p).start()
-
-    near_copy(0).start()
-    start_back(3)
-    start_far(6)
-    near_copy(1).start()
-    start_back(4)
-    start_far(7)
-    near_copy(2).start()
-    start_back(5)
-    near_copy(3).start()
-    near_copy(4).start()
+        def _(q=q):
+            back_copy(q).start()
+
+        if p < 2:
+            @pl.when(has_far)
+            def _(p=p):
+                far_copy(6 + p).start()
 
     @pl.when(core == 1)
     def _():
@@ -196,9 +195,9 @@
 
     for load in load_small:
         load.start()
-    load_sums.start()
     for u in range(tiles):
         link_copy(u).start()
+    load_sums.start()
     load_dosage.start()
 
     other_core = {"anc": a + 1 - 2 * core}
@@ -216,41 +215,48 @@
         device_id=other_core, device_id_type=MESH,
     )
 
-    chunk = unit
-
-    def widen(slot, p, odd):
-        at, size = piece(p, odd)
-
+    def clear(first, last):
         def part(i, carry):
-            r = pl.multiple_of(at + i * chunk, chunk)
-            extf[pl.ds(pl.multiple_of(slot * snps + r, chunk), chunk), :] = ext[slot, pl.ds(r, chunk), :].astype(F32)
+            at = pl.multiple_of(first + i * unit, unit)
+            field[pl.ds(at, unit), :] = jnp.zeros((unit, traits_here), F32)
             return carry
 
-        lax.fori_loop(0, size // chunk, part, 0)
-
-    def clear(slot):
-        def part(i, carry):
-            at = pl.multiple_of(slot * snps + i * chunk, chunk)
-            extf[pl.ds(at, chunk), :] = jnp.zeros((chunk, traits_here), F32)
-            return carry
-
-        lax.fori_loop(0, snps // chunk, part, 0)
-
-    for d in (-1, 1):
-        @pl.when(jnp.logical_not(in_range(g + d)))
-        def _(d=d):
-            clear(reach + d)
-
-    clear(0)
-    clear(2 * reach)
+        lax.fori_loop(0, (last - first) // unit, part, 0, unroll=4)
+
+    clear(0, own_at)
+    clear(own_at + snps, field.shape[0])
 
     for i, (d, m) in enumerate(stat_peers):
         @pl.when(jnp.logical_not(in_range(g - d)))
         def _(i=i):
             stats_in[i] = jnp.zeros(stats_in.shape[1:], F32)
 
+    @pl.when(core == 0)
+    def _():
+        pl.semaphore_wait(ready, 1)
+        up_copy.start()
+
+    @pl.when(core == 1)
+    def _():
+        up_copy.wait_recv()
+
+        def add(u, carry):
+            cols = pl.ds(pl.multiple_of(u * tile, tile), tile)
+            value = coef[:, cols] + pair[:, cols]
+            pair[:, cols] = value
+            pair_out[:, cols] = value.astype(BF16)
+            return carry
+
+        lax.fori_loop(0, tiles, add, 0, unroll=2)
+
+        @pl.when(side == 1)
+        def _():
+            pl.semaphore_wait(ready, 1)
+
+        over_copy.start()
+
     def pass_on(p):
-        if p < 3:
+        if p < 2:
             arrived(reach + even, p, 1 - parity)
 
             @pl.when(has_far)
@@ -262,55 +268,73 @@
                 arrived(reach + 2 * even, p, parity)
                 relay_near(p).start()
 
+    def widen(slot, p, odd, base):
+        at, size = piece(p, odd)
+
+        def part(i, carry):
+            r = pl.multiple_of(at + i * unit, unit)
+            field[pl.ds(pl.multiple_of(base + r, unit), unit), :] = ext[slot, pl.ds(r, unit), :].astype(F32)
+            return carry
+
+        lax.fori_loop(0, size // unit, part, 0)
+
+    def base_a(base, odd):
+        return base - odd * behind
+
+    def base_b(base, odd):
+        return base - (1 - odd) * ahead
+
+    def range_product(link, u, length, first, second=None):
+        depth = length + 128
+        within = pl.ds(pl.multiple_of(lax.rem(u, half) * tile, tile), tile)
+        rows = pl.ds(pl.multiple_of(u * tile, tile), tile)
+        begin = starts_ref[0, u] - g * snps + reach * snps
+        where, at = first
+        if second is not None:
+            here = jnp.clip(begin + width - where, 0, 1) * jnp.clip(where + length - begin, 0, 1)
+            where = second[0] + here * (where - second[0])
+            at = second[1] + here * (at - second[1])
+        skip = lax.div(jnp.clip(where - begin, 0, width - depth), 128) * 128
+        from_row = at + jnp.clip(begin + skip - where, -depth, length)
+        total = jnp.zeros((tile, traits_here), F32)
+        for c in range(0, depth, 512):
+            step = min(512, depth - c)
+            window = field[pl.ds(from_row + c, step), :].astype(BF16)
+            total = total + jnp.dot(
+                link[within, pl.ds(skip + c, step)], window, preferred_element_type=F32
+            )
+        return rows, total
+
     pass_on(0)
+    pass_on(2)
+    load_small[0].wait()
+
+    def own_tile(link, u, carry):
+        rows, total = range_product(link, u, snps, (reach * snps, own_at))
+        band[rows, :] = total
+        return carry
+
+    def each_tile(body, waits=False):
+        for i, link in enumerate(links):
+            if waits:
+                for u in range(i * half, (i + 1) * half):
+                    link_copy(u).wait()
+            lax.fori_loop(i * half, (i + 1) * half, functools.partial(body, link), 0, unroll=2)
+
+    each_tile(own_tile, waits=True)
+    pass_on(1)
     pass_on(3)
 
-    @pl.when(core == 0)
-    def _():
-        pl.semaphore_wait(ready, 1)
-        up_copy.start()
-
-    pass_on(1)
-    pass_on(4)
-
-    @pl.when(core == 1)
-    def _():
-        up_copy.wait_recv()
-
-        def add(u, carry):
-            cols = pl.ds(pl.multiple_of(u * tile, tile), tile)
-            value = coef[:, cols] + pair[:, cols]
-            pair[:, cols] = value
-            pair_out[:, cols] = value.astype(BF16)
-            return carry
-
-        lax.fori_loop(0, tiles, add, 0)
-
-        @pl.when(side == 1)
-        def _():
-            pl.semaphore_wait(ready, 1)
-
-        over_copy.start()
-
-    pass_on(2)
-    for p in range(3):
-        widen(reach + even, p, 1 - parity)
-
-    @pl.when(has_far)
-    def _():
-        arrived(reach + 2 * even, 5, parity)
-        for p in (3, 4, 5):
-            widen(reach + 2 * even, p, parity)
-
-    for p in (3, 4):
-        arrived(reach + even, p, 1 - parity)
-        widen(reach + even, p, 1 - parity)
+    for p in range(4):
+        if p > 1:
+            arrived(reach + even, p, 1 - parity)
+        widen(reach + even, p, 1 - parity, partner_at)
 
     @pl.when(has_back)
     def _():
         for p in (6, 7):
             arrived(reach - 2 * even, p, parity)
-            widen(reach - 2 * even, p, parity)
+            widen(reach - 2 * even, p, parity, back_at)
 
     @pl.when(core == 1)
     def _():
@@ -321,15 +345,50 @@
             mean[:, cols] = (pair[:, cols] + pair_in[:, cols].astype(F32)) / ancs
             return carry
 
-        lax.fori_loop(0, tiles, add, 0)
+        lax.fori_loop(0, tiles, add, 0, unroll=2)
         down_copy.start()
 
+    def side_tile(link, u, carry):
+        rows, total = range_product(
+            link, u, snps, ((reach + even) * snps, partner_at), ((reach - 2 * even) * snps, back_at)
+        )
+        band[rows, :] = band[rows, :] + total
+        return carry
+
+    each_tile(side_tile)
+
+    @pl.when(has_far)
+    def _():
+        for p in (4, 5):
+            arrived(reach + 2 * even, p, parity)
+        for p in (2, 4):
+            widen(reach + 2 * even, p, parity, base_a(far_a, parity))
+        for p in (3, 5):
+            widen(reach + 2 * even, p, parity, base_b(far_b, parity))
+
+    @pl.when(has_back)
+    def _():
+        for p in (0, 2):
+            arrived(reach - even, p, 1 - parity)
+            widen(reach - even, p, 1 - parity, base_a(across_a, 1 - parity))
+
+    def first_tile(link, u, carry):
+        rows, total = range_product(
+            link, u, ahead,
+            ((reach - even) * snps + (1 - parity) * behind, across_a),
+            ((reach + 2 * even) * snps + parity * behind, far_a),
+        )
+        band[rows, :] = band[rows, :] + total
+        return carry
+
+    each_tile(first_tile)
+
     @pl.when(core == 0)
     def _():
         down_copy.wait_recv()
 
     load_sums.wait()
-    for load in load_small:
+    for load in load_small[1:]:
         load.wait()
 
     def prepare(u, carry):
@@ -340,31 +399,26 @@
         )
         return carry
 
-    lax.fori_loop(0, tiles, prepare, 0)
+    lax.fori_loop(0, tiles, prepare, 0, unroll=2)
 
     @pl.when(has_back)
     def _():
-        for p in range(5):
+        for p in (1, 3):
             arrived(reach - even, p, 1 - parity)
-            widen(reach - even, p, 1 - parity)
-
-    def band_tile(u, carry):
-        link_copy(u).wait()
-        rows = pl.ds(pl.multiple_of(u * tile, tile), tile)
-        begin = jnp.clip(starts_ref[0, u] - g * snps + reach * snps, 0, extf.shape[0] - width)
-        depth = 512
-        total = jnp.zeros((tile, traits_here), F32)
-        for c in range(0, width, depth):
-            window = extf[pl.ds(begin + c, depth), :].astype(BF16)
-            total = total + jnp.dot(
-                link[rows, c:c + depth], window, preferred_element_type=F32
-            )
-        value = proposal[:, rows] - step_size * total.T
+            widen(reach - even, p, 1 - parity, base_b(across_b, 1 - parity))
+
+    def last_tile(link, u, carry):
+        rows, total = range_product(
+            link, u, behind,
+            ((reach - even) * snps + parity * ahead, across_b),
+            ((reach + 2 * even) * snps + (1 - parity) * ahead, far_b),
+        )
+        value = proposal[:, rows] - step_size * (band[rows, :] + total).T
         proposal[:, rows] = value
         row[:, rows] = jnp.sum(value * value, axis=0, keepdims=True)
         return carry
 
-    lax.fori_loop(0, tiles, band_tile, 0, unroll=2)
+    each_tile(last_tile)
 
     lanes = stats_out.shape[1]
     mine = lax.broadcasted_iota(jnp.int32, (groups, snps), 0) == ids_ref[...]
@@ -468,21 +522,21 @@
 
     score_ref[0] = lax.fori_loop(0, pairs - 1, add_part, pair_sum(pairs - 1))
 
-    for p in range(5):
+    for p in range(4):
         near_copy(p).wait_send()
 
     @pl.when(has_back)
     def _():
-        for p in (3, 4, 5):
+        for p in (2, 3, 4, 5):
             back_copy(p).wait_send()
 
     @pl.when(has_far)
     def _():
         for p in (6, 7):
             far_copy(p).wait_send()
-        for p in (0, 1, 2):
+        for p in (0, 1):
             relay_far(p).wait_send()
-        for p in (3, 4):
+        for p in (2, 3):
             relay_near(p).wait_send()
 
     @pl.when(core == 0)
@@ -536,6 +590,8 @@
     tile = snps // band_start.shape[1]
     slots = 2 * reach + 1
     pairs = genomes // 2
+    ahead = snps // 16 * 11
+    field_rows = 3 * snps + 4 * (snps + 128) + 4 * ahead + 4 * (snps - ahead) + 4 * 128
     group_reach = min(-(-longest_run // snps), genomes - 1)
     stat_n = (2 * group_reach + 1) * traits_n - 1
     lanes = -(-groups // 128) * 128
@@ -557,13 +613,15 @@
         scratch_shapes=[
             pltpu.VMEM((traits_here, snps), F32),
             pltpu.VMEM((traits_here, snps), F32),
-            pltpu.VMEM((snps, width), BF16),
+            pltpu.VMEM((snps // 2, width), BF16),
+            pltpu.VMEM((snps // 2, width), BF16),
             pltpu.SMEM(band_start.shape, jnp.int32),
             pltpu.VMEM(group_ids.shape, jnp.int32),
             pltpu.VMEM(group_weight.shape, F32),
             pltpu.VMEM((persons, snps), BF16),
             pltpu.VMEM((slots, snps, traits_here), BF16),
-            pltpu.VMEM((slots * snps, traits_here), F32),
+            pltpu.VMEM((field_rows, traits_here), F32),
+            pltpu.VMEM((snps, traits_here), F32),
             pltpu.VMEM((traits_here, snps), F32),
             pltpu.VMEM((traits_here, snps), F32),
             pltpu.VMEM((traits_here, snps), BF16),
@@ -578,7 +636,7 @@
             pltpu.VMEM((pairs - 1, traits_here, persons_per), BF16),
             pltpu.VMEM((pairs - 1, traits_here, persons_per), BF16),
             dma((4,)), dma((5,)), dma((snps // tile,)), pltpu.SemaphoreType.REGULAR,
-            dma((15,)), dma((slots, 8)), dma((3,)), dma((3,)),
+            dma((14,)), dma((slots, 8)), dma((3,)), dma((3,)),
             dma((stat_n,)), dma((stat_n,)), dma((pairs,)), dma((pairs,)), dma((pairs - 1,)), dma((pairs - 1,)),
         ],
         compiler_params=pltpu.CompilerParams(

time: 45.8 us -> 42.8 us (0.934)
  Pallas kernels: 45 us -> 42 us
    pallas_call x1, Pallas kernels: 44 us -> 41 us  [per_device(): pl.pallas_call(functools.partial(step_kernel, sizes), out_shape=out_shape...]
where the time goes in v2:
time: 42.8 us; the launch traced here: 42.6 us
  Pallas kernels  42 us (98%)
  between operations  0.64 us (1%)
    pallas_call x1, Pallas kernels, per_device(): pl.pallas_call(functools.partial(step_kernel, sizes), out_shape=out_shape...  41 us
    pallas_call x1, Pallas kernels, per_device(): pl.pallas_call(store_kernel, out_shape=out_shape, in_specs=[vmem, vmem],...  1.02 us

profile of v2, /device:TPU:0, one launch (start us, length us, event | category | flops | bytes accessed | tf_op | source)
XLA Modules:
  0.0 42.6 jit_solution(7584493326872176118)
XLA Ops:
  0.6 41.0 %shard_map.86 = (f32[1,128,2048]{2,1,0:T(8,128)S(1)}, f32[1,128,256]{2,1,0:T(8,128)S(1)}) custom-call(f32[1,128,2048]{2,1,0:T(8,128)} %coef_hbm.1, f32[1,128,2048]{2,1,0:T(8,128)} %sums_hbm.1, bf16[1,2048,4096]{2,1,0:T(8,128)(2,1)} %link_hbm.1, s32[1,8]{1,0:T(1,128)} %starts_hbm.1, s32[1,2048]{1,0:T(1,128)} %ids_hbm.1, f32[1,16]{1,0:T(1,128)} %weight_hbm.1, ...), custom_call_target="tpu_custom_call" | custom-call | tf_op jit(solution)/shard_map/pallas_call | solution.py:608
  41.6 1.0 %shard_map.87 = (f32[1,128,2048]{2,1,0:T(8,128)}, f32[1,128,256]{2,1,0:T(8,128)}) custom-call(f32[1,128,2048]{2,1,0:T(8,128)S(1)} %get-tuple-element.4.updated_in, f32[1,128,256]{2,1,0:T(8,128)S(1)} %get-tuple-element.5.score_in), custom_call_target="tpu_custom_call" | custom-call | tf_op jit(solution)/shard_map/pallas_call | solution.py:646

commit v3 on v2

--- a/solution.py
+++ b/solution.py
@@ -22,7 +22,7 @@
     sizes,
     coef_hbm, sums_hbm, link_hbm, starts_hbm, ids_hbm, weight_hbm, dosage_hbm,
     updated_ref, score_ref,
-    coef, sums, link_first, link_second, starts_ref, ids_ref, weight_ref, dosage, ext, field, band, pair, mean, pair_out, pair_in,
+    coef, sums, link_first, link_second, starts_ref, ids_ref, weight_ref, dosage, ext, field, band, mean, pair_out, pair_low, pair_in,
     proposal, low, row, stats_out, stats_in, side_out, side_in, part_out, part_in,
     coef_sem, load_sem, link_sem, ready,
     halo_send, halo_recv, pair_send, pair_recv, stats_send, stats_recv, side_send, side_recv, part_send, part_recv,
@@ -87,11 +87,11 @@
     def _():
         pl.semaphore_signal(barrier, inc=1, device_id={"anc": a + 1}, device_id_type=MESH)
 
-    @pl.when(jnp.logical_and(core == 1, side == 1))
+    @pl.when(jnp.logical_and(core == 0, side == 1))
     def _():
         pl.semaphore_signal(barrier, inc=1, device_id={"anc": a - 2}, device_id_type=MESH)
 
-    expected = expected + core + core * (1 - side)
+    expected = expected + core + (1 - core) * (1 - side)
 
     load_small = [
         pltpu.make_async_copy(starts_hbm, starts_ref, load_sem.at[0]),
@@ -113,11 +113,13 @@
     behind = snps - ahead
     deep = [r + 128 for r in (snps, ahead, behind)]
     own_at = deep[0]
-    partner_at = own_at + snps + deep[0]
-    back_at = partner_at + snps + deep[0]
-    across_a = back_at + snps + deep[0]
+    partner_a = own_at + snps + deep[0]
+    back_a = partner_a + ahead + deep[1]
+    across_a = back_a + ahead + deep[1]
     far_a = across_a + ahead + deep[1]
-    across_b = far_a + ahead + deep[1]
+    partner_b = far_a + ahead + deep[1]
+    back_b = partner_b + behind + deep[2]
+    across_b = back_b + behind + deep[2]
     far_b = across_b + behind + deep[2]
     assert far_b + behind + deep[2] == field.shape[0] and 13 * unit < far_rows <= 16 * unit
 
@@ -130,12 +132,19 @@
 
     for i in range(coef_parts):
         coef_copy(i).wait()
+        if i == coef_parts - 1:
+            for load in load_small:
+                load.start()
+            for u in range(tiles):
+                link_copy(u).start()
+            load_sums.start()
+            load_dosage.start()
         lax.fori_loop(i * tiles // coef_parts, (i + 1) * tiles // coef_parts, own_block, 0, unroll=2)
 
     pieces = [
         (5 * unit, 6 * unit), (13 * unit, 3 * unit), (0, 5 * unit), (11 * unit, 2 * unit),
         (5 * unit, 6 * unit), (13 * unit, far_rows - 13 * unit),
-        (snps - far_rows, far_rows // 2), (snps - far_rows + far_rows // 2, far_rows // 2),
+        (snps - far_rows, ahead + far_rows - snps), (ahead, behind),
     ]
 
     def piece(p, odd):
@@ -173,37 +182,23 @@
 
     pl.semaphore_wait(barrier, expected)
 
-    for p, q in ((0, 2), (1, 3), (2, 4), (3, 5)):
-        near_copy(p).start()
-
-        @pl.when(has_back)
-        def _(q=q):
-            back_copy(q).start()
-
-        if p < 2:
-            @pl.when(has_far)
-            def _(p=p):
-                far_copy(6 + p).start()
-
-    @pl.when(core == 1)
-    def _():
-        pl.semaphore_signal(ready, inc=1, device_id={"anc": a - 1}, device_id_type=MESH)
-
-    @pl.when(jnp.logical_and(core == 1, side == 0))
-    def _():
-        pl.semaphore_signal(ready, inc=1, device_id={"anc": a + 2}, device_id_type=MESH)
-
-    for load in load_small:
-        load.start()
-    for u in range(tiles):
-        link_copy(u).start()
-    load_sums.start()
-    load_dosage.start()
+    def send_halo():
+        for p, q in ((0, 2), (2, 3), (1, 4), (3, 5)):
+            near_copy(p).start()
+
+            @pl.when(has_back)
+            def _(q=q):
+                back_copy(q).start()
+
+            if q < 4:
+                @pl.when(has_far)
+                def _(q=q):
+                    far_copy(4 + q).start()
 
     other_core = {"anc": a + 1 - 2 * core}
     other_side = {"anc": lax.rem(a + 2, ancs)}
     up_copy = pltpu.make_async_remote_copy(
-        src_ref=coef, dst_ref=pair, send_sem=pair_send.at[0], recv_sem=pair_recv.at[0],
+        src_ref=pair_out, dst_ref=pair_low, send_sem=pair_send.at[0], recv_sem=pair_recv.at[0],
         device_id=other_core, device_id_type=MESH,
     )
     over_copy = pltpu.make_async_remote_copy(
@@ -215,6 +210,24 @@
         device_id=other_core, device_id_type=MESH,
     )
 
+    @pl.when(core == 0)
+    def _():
+        send_halo()
+
+        @pl.when(side == 0)
+        def _():
+            pl.semaphore_signal(ready, inc=1, device_id={"anc": a + 2}, device_id_type=MESH)
+
+    @pl.when(core == 1)
+    def _():
+        def round_tile(u, carry):
+            cols = pl.ds(pl.multiple_of(u * tile, tile), tile)
+            pair_out[:, cols] = coef[:, cols].astype(BF16)
+            return carry
+
+        lax.fori_loop(0, tiles, round_tile, 0, unroll=2)
+        up_copy.start()
+
     def clear(first, last):
         def part(i, carry):
             at = pl.multiple_of(first + i * unit, unit)
@@ -233,17 +246,12 @@
 
     @pl.when(core == 0)
     def _():
-        pl.semaphore_wait(ready, 1)
-        up_copy.start()
-
-    @pl.when(core == 1)
-    def _():
         up_copy.wait_recv()
 
         def add(u, carry):
             cols = pl.ds(pl.multiple_of(u * tile, tile), tile)
-            value = coef[:, cols] + pair[:, cols]
-            pair[:, cols] = value
+            value = coef[:, cols] + pair_low[:, cols].astype(F32)
+            mean[:, cols] = value
             pair_out[:, cols] = value.astype(BF16)
             return carry
 
@@ -305,57 +313,69 @@
             )
         return rows, total
 
-    pass_on(0)
-    pass_on(2)
-    load_small[0].wait()
-
     def own_tile(link, u, carry):
         rows, total = range_product(link, u, snps, (reach * snps, own_at))
         band[rows, :] = total
         return carry
 
-    def each_tile(body, waits=False):
-        for i, link in enumerate(links):
-            if waits:
-                for u in range(i * half, (i + 1) * half):
-                    link_copy(u).wait()
-            lax.fori_loop(i * half, (i + 1) * half, functools.partial(body, link), 0, unroll=2)
-
-    each_tile(own_tile, waits=True)
-    pass_on(1)
-    pass_on(3)
-
-    for p in range(4):
-        if p > 1:
-            arrived(reach + even, p, 1 - parity)
-        widen(reach + even, p, 1 - parity, partner_at)
-
-    @pl.when(has_back)
-    def _():
-        for p in (6, 7):
-            arrived(reach - 2 * even, p, parity)
-            widen(reach - 2 * even, p, parity, back_at)
+    def each_tile(body, parts=(0, 1)):
+        for i in parts:
+            lax.fori_loop(i * half, (i + 1) * half, functools.partial(body, links[i]), 0, unroll=2)
+
+    def own_pass(i):
+        for u in range(i * half, (i + 1) * half):
+            link_copy(u).wait()
+        each_tile(own_tile, (i,))
+
+    load_small[0].wait()
+    own_pass(0)
 
     @pl.when(core == 1)
     def _():
-        over_copy.wait_recv()
-
-        def add(u, carry):
-            cols = pl.ds(pl.multiple_of(u * tile, tile), tile)
-            mean[:, cols] = (pair[:, cols] + pair_in[:, cols].astype(F32)) / ancs
-            return carry
-
-        lax.fori_loop(0, tiles, add, 0, unroll=2)
-        down_copy.start()
-
-    def side_tile(link, u, carry):
+        pl.semaphore_wait(ready, 1)
+        send_halo()
+
+    for p in (0, 2, 1, 3):
+        pass_on(p)
+    own_pass(1)
+
+    @pl.when(core == 0)
+    def _():
+        near_copy(3).wait_send()
+
+        @pl.when(has_far)
+        def _():
+            relay_far(0).wait_send()
+            relay_near(2).wait_send()
+
+        pl.semaphore_signal(ready, inc=1, device_id=other_core, device_id_type=MESH)
+
+    def side_product(link, u, carry, length, offsets, bases):
         rows, total = range_product(
-            link, u, snps, ((reach + even) * snps, partner_at), ((reach - 2 * even) * snps, back_at)
+            link, u, length,
+            ((reach + even) * snps + offsets[1], bases[0]), ((reach - 2 * even) * snps + offsets[0], bases[1]),
         )
         band[rows, :] = band[rows, :] + total
         return carry
 
-    each_tile(side_tile)
+    starts_a = (parity * behind, (1 - parity) * behind)
+    starts_b = ((1 - parity) * ahead, parity * ahead)
+
+    for pieces_here, piece_back, base_of, bases, length, offsets in (
+        ((0, 2), 6, base_a, (partner_a, back_a), ahead, starts_a),
+        ((1, 3), 7, base_b, (partner_b, back_b), behind, starts_b),
+    ):
+        for p in pieces_here:
+            if p > 1:
+                arrived(reach + even, p, 1 - parity)
+            widen(reach + even, p, 1 - parity, base_of(bases[0], 1 - parity))
+
+        @pl.when(has_back)
+        def _():
+            arrived(reach - 2 * even, piece_back, parity)
+            widen(reach - 2 * even, piece_back, parity, base_of(bases[1], parity))
+
+        each_tile(functools.partial(side_product, length=length, offsets=offsets, bases=bases))
 
     @pl.when(has_far)
     def _():
@@ -375,8 +395,7 @@
     def first_tile(link, u, carry):
         rows, total = range_product(
             link, u, ahead,
-            ((reach - even) * snps + (1 - parity) * behind, across_a),
-            ((reach + 2 * even) * snps + parity * behind, far_a),
+            ((reach - even) * snps + starts_a[1], across_a), ((reach + 2 * even) * snps + starts_a[0], far_a),
         )
         band[rows, :] = band[rows, :] + total
         return carry
@@ -384,6 +403,18 @@
     each_tile(first_tile)
 
     @pl.when(core == 0)
+    def _():
+        over_copy.wait_recv()
+
+        def add(u, carry):
+            cols = pl.ds(pl.multiple_of(u * tile, tile), tile)
+            mean[:, cols] = (mean[:, cols] + pair_in[:, cols].astype(F32)) / ancs
+            return carry
+
+        lax.fori_loop(0, tiles, add, 0, unroll=2)
+        down_copy.start()
+
+    @pl.when(core == 1)
     def _():
         down_copy.wait_recv()
 
@@ -410,8 +441,7 @@
     def last_tile(link, u, carry):
         rows, total = range_product(
             link, u, behind,
-            ((reach - even) * snps + parity * ahead, across_b),
-            ((reach + 2 * even) * snps + (1 - parity) * ahead, far_b),
+            ((reach - even) * snps + starts_b[1], across_b), ((reach + 2 * even) * snps + starts_b[0], far_b),
         )
         value = proposal[:, rows] - step_size * (band[rows, :] + total).T
         proposal[:, rows] = value
@@ -475,8 +505,15 @@
     own_side, other_side_g = parity, lax.rem(near, 2)
 
     def pair_at(i):
-        k = pairs // 2 + (1 - 2 * lax.rem(i, 2)) * ((i + 1) // 2)
-        return lax.rem(g // 2 + k + pairs, pairs)
+        here = g // 2
+        below, above = here, pairs - 1 - here
+        wide = jnp.maximum(below, above)
+        single = wide - jnp.minimum(below, above)
+        up = 2 * jnp.clip(above - below, 0, 1) - 1
+        alone = jnp.clip(single - i, 0, 1)
+        two = jnp.maximum(i - single, 0)
+        away = alone * (wide - i) + (1 - alone) * (wide - single - lax.div(two, 2))
+        return here + up * (1 - 2 * (1 - alone) * lax.rem(two, 2)) * away
 
     def partial(person):
         at = pl.ds(pl.multiple_of(person * persons_per, persons_per), persons_per)
@@ -492,10 +529,12 @@
         )
 
     def part_copy(i):
+        to = pair_at(i)
+        slot = lax.rem(g // 2 - to + pairs, pairs) - 1
         return pltpu.make_async_remote_copy(
-            src_ref=part_out.at[i], dst_ref=part_in.at[i],
-            send_sem=part_send.at[i], recv_sem=part_recv.at[i],
-            device_id={"genome": 2 * pair_at(i) + own_side}, device_id_type=MESH,
+            src_ref=part_out.at[i], dst_ref=part_in.at[slot],
+            send_sem=part_send.at[i], recv_sem=part_recv.at[slot],
+            device_id={"genome": 2 * to + own_side}, device_id_type=MESH,
         )
 
     def send_side(i, carry):
@@ -516,13 +555,20 @@
     lax.fori_loop(0, pairs, send_side, 0)
     lax.fori_loop(0, pairs - 1, send_part, 0)
 
+    def part_arrived(i):
+        return pltpu.make_async_remote_copy(
+            src_ref=part_out.at[i], dst_ref=part_in.at[i],
+            send_sem=part_send.at[i], recv_sem=part_recv.at[i],
+            device_id={"genome": near}, device_id_type=MESH,
+        )
+
     def add_part(i, total):
-        part_copy(i).wait_recv()
+        part_arrived(i).wait_recv()
         return total + part_in[i].astype(F32)
 
     score_ref[0] = lax.fori_loop(0, pairs - 1, add_part, pair_sum(pairs - 1))
 
-    for p in range(4):
+    for p in range(3):
         near_copy(p).wait_send()
 
     @pl.when(has_back)
@@ -534,16 +580,21 @@
     def _():
         for p in (6, 7):
             far_copy(p).wait_send()
-        for p in (0, 1):
-            relay_far(p).wait_send()
-        for p in (2, 3):
-            relay_near(p).wait_send()
+        relay_far(1).wait_send()
+        relay_near(3).wait_send()
+
+    @pl.when(core == 1)
+    def _():
+        near_copy(3).wait_send()
+
+        @pl.when(has_far)
+        def _():
+            relay_far(0).wait_send()
+            relay_near(2).wait_send()
+
+        up_copy.wait_send()
 
     @pl.when(core == 0)
-    def _():
-        up_copy.wait_send()
-
-    @pl.when(core == 1)
     def _():
         over_copy.wait_send()
         down_copy.wait_send()
@@ -591,7 +642,7 @@
     slots = 2 * reach + 1
     pairs = genomes // 2
     ahead = snps // 16 * 11
-    field_rows = 3 * snps + 4 * (snps + 128) + 4 * ahead + 4 * (snps - ahead) + 4 * 128
+    field_rows = snps + 2 * (snps + 128) + 8 * snps + 8 * 128
     group_reach = min(-(-longest_run // snps), genomes - 1)
     stat_n = (2 * group_reach + 1) * traits_n - 1
     lanes = -(-groups // 128) * 128
@@ -623,7 +674,7 @@
             pltpu.VMEM((field_rows, traits_here), F32),
             pltpu.VMEM((snps, traits_here), F32),
             pltpu.VMEM((traits_here, snps), F32),
-            pltpu.VMEM((traits_here, snps), F32),
+            pltpu.VMEM((traits_here, snps), BF16),
             pltpu.VMEM((traits_here, snps), BF16),
             pltpu.VMEM((traits_here, snps), BF16),
             pltpu.VMEM((traits_here, snps), F32),

time: 42.8 us -> 44.1 us (1.030)
  the two profiles are of different devices: /device:TPU:0 before, /device:TPU:1 now
where the time goes in v3:
time: 44.1 us; the launch traced here: 44 us
  Pallas kernels  43.3 us (98%)
  between operations  0.64 us (1%)
    pallas_call x1, Pallas kernels, per_device(): pl.pallas_call(functools.partial(step_kernel, sizes), out_shape=out_shape...  42.3 us
    pallas_call x1, Pallas kernels, per_device(): pl.pallas_call(store_kernel, out_shape=out_shape, in_specs=[vmem, vmem],...  1.02 us

profile of v3, /device:TPU:1, one launch (start us, length us, event | category | flops | bytes accessed | tf_op | source)
XLA Modules:
  0.0 44.0 jit_solution(4859011332915556951)
XLA Ops:
  0.6 42.3 %shard_map.86 = (f32[1,128,2048]{2,1,0:T(8,128)S(1)}, f32[1,128,256]{2,1,0:T(8,128)S(1)}) custom-call(f32[1,128,2048]{2,1,0:T(8,128)} %coef_hbm.1, f32[1,128,2048]{2,1,0:T(8,128)} %sums_hbm.1, bf16[1,2048,4096]{2,1,0:T(8,128)(2,1)} %link_hbm.1, s32[1,8]{1,0:T(1,128)} %starts_hbm.1, s32[1,2048]{1,0:T(1,128)} %ids_hbm.1, f32[1,16]{1,0:T(1,128)} %weight_hbm.1, ...), custom_call_target="tpu_custom_call" | custom-call | tf_op jit(solution)/shard_map/pallas_call | solution.py:659
  43.0 1.0 %shard_map.87 = (f32[1,128,2048]{2,1,0:T(8,128)}, f32[1,128,256]{2,1,0:T(8,128)}) custom-call(f32[1,128,2048]{2,1,0:T(8,128)S(1)} %get-tuple-element.4.updated_in, f32[1,128,256]{2,1,0:T(8,128)S(1)} %get-tuple-element.5.score_in), custom_call_target="tpu_custom_call" | custom-call | tf_op jit(solution)/shard_map/pallas_call | solution.py:697

commit v4 on v3

--- a/solution.py
+++ b/solution.py
@@ -33,7 +33,7 @@
     width = link_first.shape[1]
     tiles = snps // tile
     half = tiles // 2
-    persons_per = part_out.shape[2]
+    persons_per = dosage.shape[0] // genomes
     pairs = genomes // 2
     g = lax.axis_index("genome")
     a = lax.axis_index("anc")
@@ -111,17 +111,14 @@
     far_rows = width - tile - snps
     ahead = 11 * unit
     behind = snps - ahead
-    deep = [r + 128 for r in (snps, ahead, behind)]
-    own_at = deep[0]
-    partner_a = own_at + snps + deep[0]
-    back_a = partner_a + ahead + deep[1]
-    across_a = back_a + ahead + deep[1]
-    far_a = across_a + ahead + deep[1]
-    partner_b = far_a + ahead + deep[1]
-    back_b = partner_b + behind + deep[2]
-    across_b = back_b + behind + deep[2]
-    far_b = across_b + behind + deep[2]
-    assert far_b + behind + deep[2] == field.shape[0] and 13 * unit < far_rows <= 16 * unit
+    ahead = 11 * unit
+    behind = snps - ahead
+    own_at = snps + 128
+    at_a = [own_at + 2 * snps + 128 + i * (2 * ahead + 128) for i in range(4)]
+    at_b = [at_a[3] + 2 * ahead + 128 + i * (2 * behind + 128) for i in range(4)]
+    assert at_b[3] + 2 * behind + 128 == field.shape[0] and 13 * unit < far_rows <= 16 * unit
+    first_a = (parity * behind, (1 - parity) * behind)
+    first_b = ((1 - parity) * ahead, parity * ahead)
 
     def own_block(u, carry):
         cols = pl.ds(pl.multiple_of(u * tile, tile), tile)
@@ -182,8 +179,10 @@
 
     pl.semaphore_wait(barrier, expected)
 
-    def send_halo():
-        for p, q in ((0, 2), (2, 3), (1, 4), (3, 5)):
+    rounds = ((0, 2), (2, 3), (1, 4), (3, 5))
+
+    def send_halo(rounds_here):
+        for p, q in rounds_here:
             near_copy(p).start()
 
             @pl.when(has_back)
@@ -210,9 +209,11 @@
         device_id=other_core, device_id_type=MESH,
     )
 
+    send_halo(rounds[:1])
+
     @pl.when(core == 0)
     def _():
-        send_halo()
+        send_halo(rounds[1:])
 
         @pl.when(side == 0)
         def _():
@@ -276,24 +277,20 @@
                 arrived(reach + 2 * even, p, parity)
                 relay_near(p).start()
 
-    def widen(slot, p, odd, base):
-        at, size = piece(p, odd)
-
-        def part(i, carry):
-            r = pl.multiple_of(at + i * unit, unit)
+    def widen(slot, p, same, i):
+        at, size = piece(p, parity if same else 1 - parity)
+        in_a = p in (0, 2, 4, 6)
+        base = at_a[i] - first_a[1 - same] if in_a else at_b[i] - first_b[1 - same]
+
+        def part(k, carry):
+            r = pl.multiple_of(at + k * unit, unit)
             field[pl.ds(pl.multiple_of(base + r, unit), unit), :] = ext[slot, pl.ds(r, unit), :].astype(F32)
             return carry
 
         lax.fori_loop(0, size // unit, part, 0)
 
-    def base_a(base, odd):
-        return base - odd * behind
-
-    def base_b(base, odd):
-        return base - (1 - odd) * ahead
-
     def range_product(link, u, length, first, second=None):
-        depth = length + 128
+        deep = length + 128
         within = pl.ds(pl.multiple_of(lax.rem(u, half) * tile, tile), tile)
         rows = pl.ds(pl.multiple_of(u * tile, tile), tile)
         begin = starts_ref[0, u] - g * snps + reach * snps
@@ -302,25 +299,25 @@
             here = jnp.clip(begin + width - where, 0, 1) * jnp.clip(where + length - begin, 0, 1)
             where = second[0] + here * (where - second[0])
             at = second[1] + here * (at - second[1])
-        skip = lax.div(jnp.clip(where - begin, 0, width - depth), 128) * 128
-        from_row = at + jnp.clip(begin + skip - where, -depth, length)
+        skip = lax.div(jnp.clip(where - begin, 0, width - deep), 128) * 128
+        from_row = at + jnp.clip(begin + skip - where, -deep, length)
         total = jnp.zeros((tile, traits_here), F32)
-        for c in range(0, depth, 512):
-            step = min(512, depth - c)
+        for c in range(0, deep, 512):
+            step = min(512, deep - c)
             window = field[pl.ds(from_row + c, step), :].astype(BF16)
             total = total + jnp.dot(
                 link[within, pl.ds(skip + c, step)], window, preferred_element_type=F32
             )
         return rows, total
 
+    def each_tile(body, parts=(0, 1), unroll=2):
+        for i in parts:
+            lax.fori_loop(i * half, (i + 1) * half, functools.partial(body, links[i]), 0, unroll=unroll)
+
     def own_tile(link, u, carry):
         rows, total = range_product(link, u, snps, (reach * snps, own_at))
         band[rows, :] = total
         return carry
-
-    def each_tile(body, parts=(0, 1)):
-        for i in parts:
-            lax.fori_loop(i * half, (i + 1) * half, functools.partial(body, links[i]), 0, unroll=2)
 
     def own_pass(i):
         for u in range(i * half, (i + 1) * half):
@@ -330,77 +327,78 @@
     load_small[0].wait()
     own_pass(0)
 
+    @pl.when(core == 0)
+    def _():
+        pass_on(0)
+        pass_on(2)
+
+    own_pass(1)
+
+    @pl.when(core == 0)
+    def _():
+        pass_on(1)
+        pass_on(3)
+        pl.semaphore_signal(ready, inc=1, device_id=other_core, device_id_type=MESH)
+
     @pl.when(core == 1)
     def _():
         pl.semaphore_wait(ready, 1)
-        send_halo()
-
-    for p in (0, 2, 1, 3):
-        pass_on(p)
-    own_pass(1)
-
-    @pl.when(core == 0)
-    def _():
-        near_copy(3).wait_send()
-
+        send_halo(rounds[1:])
+        pass_on(0)
+        pass_on(2)
+
+    def pair_product(link, u, slots_here, i, in_a):
+        length, firsts, bases = (ahead, first_a, at_a) if in_a else (behind, first_b, at_b)
+        return range_product(
+            link, u, length,
+            (slots_here[0] * snps + firsts[1], bases[i]), (slots_here[1] * snps + firsts[0], bases[i + 1]),
+        )
+
+    beside = (reach + even, reach - 2 * even)
+    beyond = (reach - even, reach + 2 * even)
+
+    def add_tile(link, u, carry, slots_here, i, in_a):
+        rows, total = pair_product(link, u, slots_here, i, in_a)
+        band[rows, :] = band[rows, :] + total
+        return carry
+
+    def beside_pass(in_a):
+        for p in (0, 2) if in_a else (1, 3):
+            widen(beside[0], p, 0, 0)
+
+        @pl.when(has_back)
+        def _():
+            p = 6 if in_a else 7
+            arrived(beside[1], p, parity)
+            widen(beside[1], p, 1, 1)
+
+        each_tile(functools.partial(add_tile, slots_here=beside, i=0, in_a=in_a), unroll=4)
+
+    def beyond_ready(in_a):
         @pl.when(has_far)
         def _():
-            relay_far(0).wait_send()
-            relay_near(2).wait_send()
-
-        pl.semaphore_signal(ready, inc=1, device_id=other_core, device_id_type=MESH)
-
-    def side_product(link, u, carry, length, offsets, bases):
-        rows, total = range_product(
-            link, u, length,
-            ((reach + even) * snps + offsets[1], bases[0]), ((reach - 2 * even) * snps + offsets[0], bases[1]),
-        )
-        band[rows, :] = band[rows, :] + total
-        return carry
-
-    starts_a = (parity * behind, (1 - parity) * behind)
-    starts_b = ((1 - parity) * ahead, parity * ahead)
-
-    for pieces_here, piece_back, base_of, bases, length, offsets in (
-        ((0, 2), 6, base_a, (partner_a, back_a), ahead, starts_a),
-        ((1, 3), 7, base_b, (partner_b, back_b), behind, starts_b),
-    ):
-        for p in pieces_here:
-            if p > 1:
-                arrived(reach + even, p, 1 - parity)
-            widen(reach + even, p, 1 - parity, base_of(bases[0], 1 - parity))
+            arrived(beyond[1], 4 if in_a else 5, parity)
+            for p in (2, 4) if in_a else (3, 5):
+                widen(beyond[1], p, 1, 3)
 
         @pl.when(has_back)
         def _():
-            arrived(reach - 2 * even, piece_back, parity)
-            widen(reach - 2 * even, piece_back, parity, base_of(bases[1], parity))
-
-        each_tile(functools.partial(side_product, length=length, offsets=offsets, bases=bases))
-
-    @pl.when(has_far)
-    def _():
-        for p in (4, 5):
-            arrived(reach + 2 * even, p, parity)
-        for p in (2, 4):
-            widen(reach + 2 * even, p, parity, base_a(far_a, parity))
-        for p in (3, 5):
-            widen(reach + 2 * even, p, parity, base_b(far_b, parity))
-
-    @pl.when(has_back)
-    def _():
-        for p in (0, 2):
-            arrived(reach - even, p, 1 - parity)
-            widen(reach - even, p, 1 - parity, base_a(across_a, 1 - parity))
-
-    def first_tile(link, u, carry):
-        rows, total = range_product(
-            link, u, ahead,
-            ((reach - even) * snps + starts_a[1], across_a), ((reach + 2 * even) * snps + starts_a[0], far_a),
-        )
-        band[rows, :] = band[rows, :] + total
-        return carry
-
-    each_tile(first_tile)
+            for p in (0, 2) if in_a else (1, 3):
+                arrived(beyond[0], p, 1 - parity)
+                widen(beyond[0], p, 0, 2)
+
+    arrived(beside[0], 2, 1 - parity)
+    beside_pass(True)
+
+    @pl.when(core == 1)
+    def _():
+        pass_on(1)
+        pass_on(3)
+
+    arrived(beside[0], 3, 1 - parity)
+    beside_pass(False)
+    beyond_ready(True)
+    each_tile(functools.partial(add_tile, slots_here=beyond, i=2, in_a=True), unroll=4)
 
     @pl.when(core == 0)
     def _():
@@ -432,23 +430,16 @@
 
     lax.fori_loop(0, tiles, prepare, 0, unroll=2)
 
-    @pl.when(has_back)
-    def _():
-        for p in (1, 3):
-            arrived(reach - even, p, 1 - parity)
-            widen(reach - even, p, 1 - parity, base_b(across_b, 1 - parity))
+    beyond_ready(False)
 
     def last_tile(link, u, carry):
-        rows, total = range_product(
-            link, u, behind,
-            ((reach - even) * snps + starts_b[1], across_b), ((reach + 2 * even) * snps + starts_b[0], far_b),
-        )
+        rows, total = pair_product(link, u, beyond, 2, False)
         value = proposal[:, rows] - step_size * (band[rows, :] + total).T
         proposal[:, rows] = value
         row[:, rows] = jnp.sum(value * value, axis=0, keepdims=True)
         return carry
 
-    each_tile(last_tile)
+    each_tile(last_tile, unroll=4)
 
     lanes = stats_out.shape[1]
     mine = lax.broadcasted_iota(jnp.int32, (groups, snps), 0) == ids_ref[...]
@@ -515,8 +506,11 @@
         away = alone * (wide - i) + (1 - alone) * (wide - single - lax.div(two, 2))
         return here + up * (1 - 2 * (1 - alone) * lax.rem(two, 2)) * away
 
-    def partial(person):
-        at = pl.ds(pl.multiple_of(person * persons_per, persons_per), persons_per)
+    cuts = side_out.shape[0] // pairs
+    sub = side_out.shape[2]
+
+    def partial(person, i):
+        at = pl.ds(pl.multiple_of(person * persons_per + lax.rem(i, cuts) * sub, sub), sub)
         return lax.dot_general(
             low[...], dosage[at, :], (((1,), (1,)), ((), ())), preferred_element_type=F32
         ) * scale
@@ -529,31 +523,13 @@
         )
 
     def part_copy(i):
-        to = pair_at(i)
-        slot = lax.rem(g // 2 - to + pairs, pairs) - 1
+        to = pair_at(i // cuts)
+        slot = (lax.rem(g // 2 - to + pairs, pairs) - 1) * cuts + lax.rem(i, cuts)
         return pltpu.make_async_remote_copy(
             src_ref=part_out.at[i], dst_ref=part_in.at[slot],
             send_sem=part_send.at[i], recv_sem=part_recv.at[slot],
             device_id={"genome": 2 * to + own_side}, device_id_type=MESH,
         )
-
-    def send_side(i, carry):
-        side_out[i] = partial(2 * pair_at(i) + other_side_g).astype(BF16)
-        side_copy(i).start()
-        return carry
-
-    def pair_sum(i):
-        mine_here = partial(2 * pair_at(i) + own_side)
-        side_copy(i).wait_recv()
-        return mine_here + side_in[i].astype(F32)
-
-    def send_part(i, carry):
-        part_out[i] = pair_sum(i).astype(BF16)
-        part_copy(i).start()
-        return carry
-
-    lax.fori_loop(0, pairs, send_side, 0)
-    lax.fori_loop(0, pairs - 1, send_part, 0)
 
     def part_arrived(i):
         return pltpu.make_async_remote_copy(
@@ -562,13 +538,34 @@
             device_id={"genome": near}, device_id_type=MESH,
         )
 
-    def add_part(i, total):
-        part_arrived(i).wait_recv()
-        return total + part_in[i].astype(F32)
-
-    score_ref[0] = lax.fori_loop(0, pairs - 1, add_part, pair_sum(pairs - 1))
-
-    for p in range(3):
+    def send_side(i, carry):
+        side_out[i] = partial(2 * pair_at(i // cuts) + other_side_g, i).astype(BF16)
+        side_copy(i).start()
+        return carry
+
+    def pair_sum(i):
+        mine_here = partial(2 * pair_at(i // cuts) + own_side, i)
+        side_copy(i).wait_recv()
+        return mine_here + side_in[i].astype(F32)
+
+    def send_part(i, carry):
+        part_out[i] = pair_sum(i).astype(BF16)
+        part_copy(i).start()
+        return carry
+
+    n_side, n_part = pairs * cuts, (pairs - 1) * cuts
+    lax.fori_loop(0, n_side, send_side, 0)
+    lax.fori_loop(0, n_part, send_part, 0)
+
+    totals = [pair_sum(n_part + c) for c in range(cuts)]
+    for c in range(cuts):
+        def add_part(k, total, c=c):
+            part_arrived(k * cuts + c).wait_recv()
+            return total + part_in[k * cuts + c].astype(F32)
+
+        score_ref[0, :, c * sub:(c + 1) * sub] = lax.fori_loop(0, pairs - 1, add_part, totals[c])
+
+    for p in range(4):
         near_copy(p).wait_send()
 
     @pl.when(has_back)
@@ -580,18 +577,13 @@
     def _():
         for p in (6, 7):
             far_copy(p).wait_send()
-        relay_far(1).wait_send()
-        relay_near(3).wait_send()
+        for p in (0, 1):
+            relay_far(p).wait_send()
+        for p in (2, 3):
+            relay_near(p).wait_send()
 
     @pl.when(core == 1)
     def _():
-        near_copy(3).wait_send()
-
-        @pl.when(has_far)
-        def _():
-            relay_far(0).wait_send()
-            relay_near(2).wait_send()
-
         up_copy.wait_send()
 
     @pl.when(core == 0)
@@ -612,8 +604,8 @@
         part_copy(i).wait_send()
         return carry
 
-    lax.fori_loop(0, pairs, sent_side, 0)
-    lax.fori_loop(0, pairs - 1, sent_part, 0)
+    lax.fori_loop(0, n_side, sent_side, 0)
+    lax.fori_loop(0, n_part, sent_part, 0)
 
 
 def store_kernel(updated_in, score_in, updated_out, score_out, sem):
@@ -641,9 +633,10 @@
     tile = snps // band_start.shape[1]
     slots = 2 * reach + 1
     pairs = genomes // 2
-    ahead = snps // 16 * 11
-    field_rows = snps + 2 * (snps + 128) + 8 * snps + 8 * 128
+    field_rows = 11 * snps + 10 * 128
     group_reach = min(-(-longest_run // snps), genomes - 1)
+    cuts = max(1, persons_per // 128)
+    n_side, n_part = pairs * cuts, (pairs - 1) * cuts
     stat_n = (2 * group_reach + 1) * traits_n - 1
     lanes = -(-groups // 128) * 128
     sizes = (genomes, ancs, traits_n, reach, tile, groups)
@@ -682,13 +675,13 @@
             pltpu.VMEM((1, snps), F32),
             pltpu.VMEM((2, lanes), F32),
             pltpu.VMEM((stat_n, 2, lanes), F32),
-            pltpu.VMEM((pairs, traits_here, persons_per), BF16),
-            pltpu.VMEM((pairs, traits_here, persons_per), BF16),
-            pltpu.VMEM((pairs - 1, traits_here, persons_per), BF16),
-            pltpu.VMEM((pairs - 1, traits_here, persons_per), BF16),
+            pltpu.VMEM((n_side, traits_here, persons_per // cuts), BF16),
+            pltpu.VMEM((n_side, traits_here, persons_per // cuts), BF16),
+            pltpu.VMEM((n_part, traits_here, persons_per // cuts), BF16),
+            pltpu.VMEM((n_part, traits_here, persons_per // cuts), BF16),
             dma((4,)), dma((5,)), dma((snps // tile,)), pltpu.SemaphoreType.REGULAR,
             dma((14,)), dma((slots, 8)), dma((3,)), dma((3,)),
-            dma((stat_n,)), dma((stat_n,)), dma((pairs,)), dma((pairs,)), dma((pairs - 1,)), dma((pairs - 1,)),
+            dma((stat_n,)), dma((stat_n,)), dma((n_side,)), dma((n_side,)), dma((n_part,)), dma((n_part,)),
         ],
         compiler_params=pltpu.CompilerParams(
             collective_id=0, has_side_effects=True, vmem_limit_bytes=52 * 1024 * 1024

time: 44.1 us -> 38.3 us (0.87)
  Pallas kernels: 43.3 us -> 37.5 us
    pallas_call x1, Pallas kernels: 42.3 us -> 36.4 us  [per_device(): pl.pallas_call(functools.partial(step_kernel, sizes), out_shape=out_shape...]
where the time goes in v4:
time: 38.3 us; the launch traced here: 38.1 us
  Pallas kernels  37.5 us (98%)
  between operations  0.64 us (2%)
    pallas_call x1, Pallas kernels, per_device(): pl.pallas_call(functools.partial(step_kernel, sizes), out_shape=out_shape...  36.4 us
    pallas_call x1, Pallas kernels, per_device(): pl.pallas_call(store_kernel, out_shape=out_shape, in_specs=[vmem, vmem],...  1.02 us

profile of v4, /device:TPU:1, one launch (start us, length us, event | category | flops | bytes accessed | tf_op | source)
XLA Modules:
  0.0 38.1 jit_solution(12648982904484381383)
XLA Ops:
  0.6 36.4 %shard_map.86 = (f32[1,128,2048]{2,1,0:T(8,128)S(1)}, f32[1,128,256]{2,1,0:T(8,128)S(1)}) custom-call(f32[1,128,2048]{2,1,0:T(8,128)} %coef_hbm.1, f32[1,128,2048]{2,1,0:T(8,128)} %sums_hbm.1, bf16[1,2048,4096]{2,1,0:T(8,128)(2,1)} %link_hbm.1, s32[1,8]{1,0:T(1,128)} %starts_hbm.1, s32[1,2048]{1,0:T(1,128)} %ids_hbm.1, f32[1,16]{1,0:T(1,128)} %weight_hbm.1, ...), custom_call_target="tpu_custom_call" | custom-call | tf_op jit(solution)/shard_map/pallas_call | solution.py:652
  37.1 1.0 %shard_map.87 = (f32[1,128,2048]{2,1,0:T(8,128)}, f32[1,128,256]{2,1,0:T(8,128)}) custom-call(f32[1,128,2048]{2,1,0:T(8,128)S(1)} %get-tuple-element.4.updated_in, f32[1,128,256]{2,1,0:T(8,128)S(1)} %get-tuple-element.5.score_in), custom_call_target="tpu_custom_call" | custom-call | tf_op jit(solution)/shard_map/pallas_call | solution.py:690

commit v5 on v4

--- a/solution.py
+++ b/solution.py
@@ -179,20 +179,18 @@
 
     pl.semaphore_wait(barrier, expected)
 
-    rounds = ((0, 2), (2, 3), (1, 4), (3, 5))
-
-    def send_halo(rounds_here):
-        for p, q in rounds_here:
-            near_copy(p).start()
-
-            @pl.when(has_back)
-            def _(q=q):
-                back_copy(q).start()
-
-            if q < 4:
+    def send_halo(nears, backs, fars):
+        for k in range(4):
+            for p in nears[k:k + 1]:
+                near_copy(p).start()
+            for p in backs[k:k + 1]:
+                @pl.when(has_back)
+                def _(p=p):
+                    back_copy(p).start()
+            for p in fars[k:k + 1]:
                 @pl.when(has_far)
-                def _(q=q):
-                    far_copy(4 + q).start()
+                def _(p=p):
+                    far_copy(p).start()
 
     other_core = {"anc": a + 1 - 2 * core}
     other_side = {"anc": lax.rem(a + 2, ancs)}
@@ -209,11 +207,9 @@
         device_id=other_core, device_id_type=MESH,
     )
 
-    send_halo(rounds[:1])
-
     @pl.when(core == 0)
     def _():
-        send_halo(rounds[1:])
+        send_halo((0, 2, 1, 3), (2, 3, 4, 5), (6, 7))
 
         @pl.when(side == 0)
         def _():
@@ -221,6 +217,8 @@
 
     @pl.when(core == 1)
     def _():
+        send_halo((0,), (2,), (6,))
+
         def round_tile(u, carry):
             cols = pl.ds(pl.multiple_of(u * tile, tile), tile)
             pair_out[:, cols] = coef[:, cols].astype(BF16)
@@ -336,14 +334,14 @@
 
     @pl.when(core == 0)
     def _():
-        pass_on(1)
-        pass_on(3)
         pl.semaphore_signal(ready, inc=1, device_id=other_core, device_id_type=MESH)
 
     @pl.when(core == 1)
     def _():
         pl.semaphore_wait(ready, 1)
-        send_halo(rounds[1:])
+        send_halo((2,), (), ())
+        pl.semaphore_wait(ready, 1)
+        send_halo((1, 3), (3, 4, 5), (7,))
         pass_on(0)
         pass_on(2)
 
@@ -389,11 +387,12 @@
 
     arrived(beside[0], 2, 1 - parity)
     beside_pass(True)
-
-    @pl.when(core == 1)
-    def _():
-        pass_on(1)
-        pass_on(3)
+    pass_on(1)
+    pass_on(3)
+
+    @pl.when(core == 0)
+    def _():
+        pl.semaphore_signal(ready, inc=1, device_id=other_core, device_id_type=MESH)
 
     arrived(beside[0], 3, 1 - parity)
     beside_pass(False)
@@ -430,6 +429,14 @@
 
     lax.fori_loop(0, tiles, prepare, 0, unroll=2)
 
+    lanes = stats_out.shape[1]
+    mine = lax.broadcasted_iota(jnp.int32, (groups, snps), 0) == ids_ref[...]
+    counts = jnp.sum(jnp.where(mine, 1.0, 0.0), axis=1, keepdims=True)
+    on_lane = lax.broadcasted_iota(jnp.int32, (groups, lanes), 0) == lax.broadcasted_iota(
+        jnp.int32, (groups, lanes), 1
+    )
+    stats_out[1:2, :] = jnp.sum(jnp.where(on_lane, counts, 0.0), axis=0, keepdims=True)
+
     beyond_ready(False)
 
     def last_tile(link, u, carry):
@@ -441,15 +448,8 @@
 
     each_tile(last_tile, unroll=4)
 
-    lanes = stats_out.shape[1]
-    mine = lax.broadcasted_iota(jnp.int32, (groups, snps), 0) == ids_ref[...]
     squares = jnp.sum(jnp.where(mine, row[...], 0.0), axis=1, keepdims=True)
-    counts = jnp.sum(jnp.where(mine, 1.0, 0.0), axis=1, keepdims=True)
-    on_lane = lax.broadcasted_iota(jnp.int32, (groups, lanes), 0) == lax.broadcasted_iota(
-        jnp.int32, (groups, lanes), 1
-    )
     stats_out[0:1, :] = jnp.sum(jnp.where(on_lane, squares, 0.0), axis=0, keepdims=True)
-    stats_out[1:2, :] = jnp.sum(jnp.where(on_lane, counts, 0.0), axis=0, keepdims=True)
 
     def stats_copy(i):
         d, m = stat_peers[i]
@@ -497,73 +497,70 @@
 
     def pair_at(i):
         here = g // 2
-        below, above = here, pairs - 1 - here
-        wide = jnp.maximum(below, above)
-        single = wide - jnp.minimum(below, above)
-        up = 2 * jnp.clip(above - below, 0, 1) - 1
-        alone = jnp.clip(single - i, 0, 1)
-        two = jnp.maximum(i - single, 0)
-        away = alone * (wide - i) + (1 - alone) * (wide - single - lax.div(two, 2))
-        return here + up * (1 - 2 * (1 - alone) * lax.rem(two, 2)) * away
-
-    cuts = side_out.shape[0] // pairs
-    sub = side_out.shape[2]
-
-    def partial(person, i):
-        at = pl.ds(pl.multiple_of(person * persons_per + lax.rem(i, cuts) * sub, sub), sub)
+        is_last = jnp.clip(i - (pairs - 2), 0, 1)
+        return (1 - is_last) * (i + jnp.clip(i - here + 1, 0, 1)) + is_last * here
+
+    cuts = side_out.shape[1]
+    sub = traits_here // cuts
+    last_pair = pairs - 1
+
+    def partial(person):
+        at = pl.ds(pl.multiple_of(person * persons_per, persons_per), persons_per)
         return lax.dot_general(
             low[...], dosage[at, :], (((1,), (1,)), ((), ())), preferred_element_type=F32
         ) * scale
 
-    def side_copy(i):
+    def side_copy(i, c):
         return pltpu.make_async_remote_copy(
-            src_ref=side_out.at[i], dst_ref=side_in.at[i],
-            send_sem=side_send.at[i], recv_sem=side_recv.at[i],
+            src_ref=side_out.at[i, c], dst_ref=side_in.at[i, c],
+            send_sem=side_send.at[i, c], recv_sem=side_recv.at[i, c],
             device_id={"genome": near}, device_id_type=MESH,
         )
 
-    def part_copy(i):
-        to = pair_at(i // cuts)
-        slot = (lax.rem(g // 2 - to + pairs, pairs) - 1) * cuts + lax.rem(i, cuts)
+    def part_copy(i, c):
+        to = pair_at(i)
+        slot = lax.rem(g // 2 - to + pairs, pairs) - 1
         return pltpu.make_async_remote_copy(
-            src_ref=part_out.at[i], dst_ref=part_in.at[slot],
-            send_sem=part_send.at[i], recv_sem=part_recv.at[slot],
+            src_ref=part_out.at[i, c], dst_ref=part_in.at[slot, c],
+            send_sem=part_send.at[i, c], recv_sem=part_recv.at[slot, c],
             device_id={"genome": 2 * to + own_side}, device_id_type=MESH,
         )
 
-    def part_arrived(i):
+    def part_arrived(i, c):
         return pltpu.make_async_remote_copy(
-            src_ref=part_out.at[i], dst_ref=part_in.at[i],
-            send_sem=part_send.at[i], recv_sem=part_recv.at[i],
+            src_ref=part_out.at[i, c], dst_ref=part_in.at[i, c],
+            send_sem=part_send.at[i, c], recv_sem=part_recv.at[i, c],
             device_id={"genome": near}, device_id_type=MESH,
         )
 
     def send_side(i, carry):
-        side_out[i] = partial(2 * pair_at(i // cuts) + other_side_g, i).astype(BF16)
-        side_copy(i).start()
-        return carry
-
-    def pair_sum(i):
-        mine_here = partial(2 * pair_at(i // cuts) + own_side, i)
-        side_copy(i).wait_recv()
-        return mine_here + side_in[i].astype(F32)
+        value = partial(2 * pair_at(i) + other_side_g).astype(BF16)
+        for c in range(cuts):
+            side_out[i, c] = value[c * sub:(c + 1) * sub]
+            side_copy(i, c).start()
+        return carry
 
     def send_part(i, carry):
-        part_out[i] = pair_sum(i).astype(BF16)
-        part_copy(i).start()
-        return carry
-
-    n_side, n_part = pairs * cuts, (pairs - 1) * cuts
-    lax.fori_loop(0, n_side, send_side, 0)
-    lax.fori_loop(0, n_part, send_part, 0)
-
-    totals = [pair_sum(n_part + c) for c in range(cuts)]
+        mine_here = partial(2 * pair_at(i) + own_side)
+        for c in range(cuts):
+            side_copy(i, c).wait_recv()
+            part_out[i, c] = (mine_here[c * sub:(c + 1) * sub] + side_in[i, c].astype(F32)).astype(BF16)
+            part_copy(i, c).start()
+        return carry
+
+    lax.fori_loop(0, pairs, send_side, 0)
+    lax.fori_loop(0, last_pair, send_part, 0)
+
+    last = partial(2 * pair_at(last_pair) + own_side)
     for c in range(cuts):
+        side_copy(last_pair, c).wait_recv()
+
         def add_part(k, total, c=c):
-            part_arrived(k * cuts + c).wait_recv()
-            return total + part_in[k * cuts + c].astype(F32)
-
-        score_ref[0, :, c * sub:(c + 1) * sub] = lax.fori_loop(0, pairs - 1, add_part, totals[c])
+            part_arrived(k, c).wait_recv()
+            return total + part_in[k, c].astype(F32)
+
+        own_total = last[c * sub:(c + 1) * sub] + side_in[last_pair, c].astype(F32)
+        score_ref[0, c * sub:(c + 1) * sub, :] = lax.fori_loop(0, pairs - 1, add_part, own_total)
 
     for p in range(4):
         near_copy(p).wait_send()
@@ -597,22 +594,26 @@
             stats_copy(i).wait_send()
 
     def sent_side(i, carry):
-        side_copy(i).wait_send()
+        for c in range(cuts):
+            side_copy(i, c).wait_send()
         return carry
 
     def sent_part(i, carry):
-        part_copy(i).wait_send()
-        return carry
-
-    lax.fori_loop(0, n_side, sent_side, 0)
-    lax.fori_loop(0, n_part, sent_part, 0)
+        for c in range(cuts):
+            part_copy(i, c).wait_send()
+        return carry
+
+    lax.fori_loop(0, pairs, sent_side, 0)
+    lax.fori_loop(0, pairs - 1, sent_part, 0)
 
 
 def store_kernel(updated_in, score_in, updated_out, score_out, sem):
-    copies = [
-        pltpu.make_async_copy(updated_in, updated_out, sem.at[0]),
-        pltpu.make_async_copy(score_in, score_out, sem.at[1]),
-    ]
+    parts = sem.shape[0] - 1
+    rows = updated_in.shape[1] // parts
+    copies = [pltpu.make_async_copy(score_in, score_out, sem.at[parts])]
+    for i in range(parts):
+        part = pl.ds(i * rows, rows)
+        copies.append(pltpu.make_async_copy(updated_in.at[:, part], updated_out.at[:, part], sem.at[i]))
     for copy in copies:
         copy.start()
     for copy in copies:
@@ -635,8 +636,7 @@
     pairs = genomes // 2
     field_rows = 11 * snps + 10 * 128
     group_reach = min(-(-longest_run // snps), genomes - 1)
-    cuts = max(1, persons_per // 128)
-    n_side, n_part = pairs * cuts, (pairs - 1) * cuts
+    cuts = 2
     stat_n = (2 * group_reach + 1) * traits_n - 1
     lanes = -(-groups // 128) * 128
     sizes = (genomes, ancs, traits_n, reach, tile, groups)
@@ -675,13 +675,13 @@
             pltpu.VMEM((1, snps), F32),
             pltpu.VMEM((2, lanes), F32),
             pltpu.VMEM((stat_n, 2, lanes), F32),
-            pltpu.VMEM((n_side, traits_here, persons_per // cuts), BF16),
-            pltpu.VMEM((n_side, traits_here, persons_per // cuts), BF16),
-            pltpu.VMEM((n_part, traits_here, persons_per // cuts), BF16),
-            pltpu.VMEM((n_part, traits_here, persons_per // cuts), BF16),
+            pltpu.VMEM((pairs, cuts, traits_here // cuts, persons_per), BF16),
+            pltpu.VMEM((pairs, cuts, traits_here // cuts, persons_per), BF16),
+            pltpu.VMEM((pairs - 1, cuts, traits_here // cuts, persons_per), BF16),
+            pltpu.VMEM((pairs - 1, cuts, traits_here // cuts, persons_per), BF16),
             dma((4,)), dma((5,)), dma((snps // tile,)), pltpu.SemaphoreType.REGULAR,
             dma((14,)), dma((slots, 8)), dma((3,)), dma((3,)),
-            dma((stat_n,)), dma((stat_n,)), dma((n_side,)), dma((n_side,)), dma((n_part,)), dma((n_part,)),
+            dma((stat_n,)), dma((stat_n,)), dma((pairs, cuts)), dma((pairs, cuts)), dma((pairs - 1, cuts)), dma((pairs - 1, cuts)),
         ],
         compiler_params=pltpu.CompilerParams(
             collective_id=0, has_side_effects=True, vmem_limit_bytes=52 * 1024 * 1024
@@ -692,7 +692,7 @@
         out_shape=out_shape,
         in_specs=[vmem, vmem],
         out_specs=(hbm, hbm),
-        scratch_shapes=[dma((2,))],
+        scratch_shapes=[dma((5,))],
     )(*(pltpu.with_memory_space_constraint(x, pltpu.VMEM) for x in (updated, scores)))
 
 

time: 38.3 us -> 38.1 us (level)
  Pallas kernels: 37.5 us -> 37 us
    pallas_call x1, Pallas kernels: 36.4 us -> 35.9 us  [per_device(): pl.pallas_call(functools.partial(step_kernel, sizes), out_shape=out_shape...]
where the time goes in v5:
time: 38.1 us; the launch traced here: 37.6 us
  Pallas kernels  37 us (97%)
  between operations  0.64 us (2%)
    pallas_call x1, Pallas kernels, per_device(): pl.pallas_call(functools.partial(step_kernel, sizes), out_shape=out_shape...  35.9 us
    pallas_call x1, Pallas kernels, per_device(): pl.pallas_call(store_kernel, out_shape=out_shape, in_specs=[vmem, vmem],...  1.05 us

profile of v5, /device:TPU:1, one launch (start us, length us, event | category | flops | bytes accessed | tf_op | source)
XLA Modules:
  0.0 37.6 jit_solution(6191348120121980496)
XLA Ops:
  0.6 35.9 %shard_map.86 = (f32[1,128,2048]{2,1,0:T(8,128)S(1)}, f32[1,128,256]{2,1,0:T(8,128)S(1)}) custom-call(f32[1,128,2048]{2,1,0:T(8,128)} %coef_hbm.1, f32[1,128,2048]{2,1,0:T(8,128)} %sums_hbm.1, bf16[1,2048,4096]{2,1,0:T(8,128)(2,1)} %link_hbm.1, s32[1,8]{1,0:T(1,128)} %starts_hbm.1, s32[1,2048]{1,0:T(1,128)} %ids_hbm.1, f32[1,16]{1,0:T(1,128)} %weight_hbm.1, ...), custom_call_target="tpu_custom_call" | custom-call | tf_op jit(solution)/shard_map/pallas_call | solution.py:652
  36.6 1.0 %shard_map.87 = (f32[1,128,2048]{2,1,0:T(8,128)}, f32[1,128,256]{2,1,0:T(8,128)}) custom-call(f32[1,128,2048]{2,1,0:T(8,128)S(1)} %get-tuple-element.4.updated_in, f32[1,128,256]{2,1,0:T(8,128)S(1)} %get-tuple-element.5.score_in), custom_call_target="tpu_custom_call" | custom-call | tf_op jit(solution)/shard_map/pallas_call | solution.py:690

commit v6 on v5

--- a/solution.py
+++ b/solution.py
@@ -396,8 +396,6 @@
 
     arrived(beside[0], 3, 1 - parity)
     beside_pass(False)
-    beyond_ready(True)
-    each_tile(functools.partial(add_tile, slots_here=beyond, i=2, in_a=True), unroll=4)
 
     @pl.when(core == 0)
     def _():
@@ -436,6 +434,9 @@
         jnp.int32, (groups, lanes), 1
     )
     stats_out[1:2, :] = jnp.sum(jnp.where(on_lane, counts, 0.0), axis=0, keepdims=True)
+
+    beyond_ready(True)
+    each_tile(functools.partial(add_tile, slots_here=beyond, i=2, in_a=True), unroll=4)
 
     beyond_ready(False)
 
@@ -483,14 +484,17 @@
     shrink = jnp.sum(jnp.where(same, shrink, 0.0), axis=1, keepdims=True)
     row[...] = jnp.sum(jnp.where(mine, shrink, 0.0), axis=0, keepdims=True)
 
-    def shrink_tile(u, carry):
+    def round_updated(u, carry):
         cols = pl.ds(pl.multiple_of(u * tile, tile), tile)
-        value = proposal[:, cols] * row[:, cols]
-        updated_ref[0, :, cols] = value
-        low[:, cols] = value.astype(BF16)
-        return carry
-
-    lax.fori_loop(0, tiles, shrink_tile, 0, unroll=2)
+        low[:, cols] = (proposal[:, cols] * row[:, cols]).astype(BF16)
+        return carry
+
+    def keep_updated(u, carry):
+        cols = pl.ds(pl.multiple_of(u * tile, tile), tile)
+        updated_ref[0, :, cols] = proposal[:, cols] * row[:, cols]
+        return carry
+
+    lax.fori_loop(0, tiles, round_updated, 0, unroll=4)
 
     scale = 1.0 / math.sqrt(snps * genomes)
     own_side, other_side_g = parity, lax.rem(near, 2)
@@ -550,6 +554,7 @@
 
     lax.fori_loop(0, pairs, send_side, 0)
     lax.fori_loop(0, last_pair, send_part, 0)
+    lax.fori_loop(0, tiles, keep_updated, 0, unroll=2)
 
     last = partial(2 * pair_at(last_pair) + own_side)
     for c in range(cuts):

time: 38.1 us -> 37.7 us (0.990)
  no operation moved by 1% of the time
where the time goes in v6:
time: 37.7 us; the launch traced here: 37.6 us
  Pallas kernels  36.9 us (98%)
  between operations  0.64 us (2%)
    pallas_call x1, Pallas kernels, per_device(): pl.pallas_call(functools.partial(step_kernel, sizes), out_shape=out_shape...  35.9 us
    pallas_call x1, Pallas kernels, per_device(): pl.pallas_call(store_kernel, out_shape=out_shape, in_specs=[vmem, vmem],...  1.05 us

profile of v6, /device:TPU:1, one launch (start us, length us, event | category | flops | bytes accessed | tf_op | source)
XLA Modules:
  0.0 37.6 jit_solution(17761367348147319655)
XLA Ops:
  0.6 35.9 %shard_map.86 = (f32[1,128,2048]{2,1,0:T(8,128)S(1)}, f32[1,128,256]{2,1,0:T(8,128)S(1)}) custom-call(f32[1,128,2048]{2,1,0:T(8,128)} %coef_hbm.1, f32[1,128,2048]{2,1,0:T(8,128)} %sums_hbm.1, bf16[1,2048,4096]{2,1,0:T(8,128)(2,1)} %link_hbm.1, s32[1,8]{1,0:T(1,128)} %starts_hbm.1, s32[1,2048]{1,0:T(1,128)} %ids_hbm.1, f32[1,16]{1,0:T(1,128)} %weight_hbm.1, ...), custom_call_target="tpu_custom_call" | custom-call | tf_op jit(solution)/shard_map/pallas_call | solution.py:657
  36.5 1.0 %shard_map.87 = (f32[1,128,2048]{2,1,0:T(8,128)}, f32[1,128,256]{2,1,0:T(8,128)}) custom-call(f32[1,128,2048]{2,1,0:T(8,128)S(1)} %get-tuple-element.4.updated_in, f32[1,128,256]{2,1,0:T(8,128)S(1)} %get-tuple-element.5.score_in), custom_call_target="tpu_custom_call" | custom-call | tf_op jit(solution)/shard_map/pallas_call | solution.py:695

commit v7 on v6

--- a/solution.py
+++ b/solution.py
@@ -320,7 +320,7 @@
     def own_pass(i):
         for u in range(i * half, (i + 1) * half):
             link_copy(u).wait()
-        each_tile(own_tile, (i,))
+        each_tile(own_tile, (i,), unroll=4)
 
     load_small[0].wait()
     own_pass(0)

time: 37.7 us -> 37.8 us (level)
  no operation moved by 1% of the time
where the time goes in v7:
time: 37.8 us; the launch traced here: 37.5 us
  Pallas kernels  36.8 us (97%)
  between operations  0.64 us (2%)
    pallas_call x1, Pallas kernels, per_device(): pl.pallas_call(functools.partial(step_kernel, sizes), out_shape=out_shape...  35.8 us
    pallas_call x1, Pallas kernels, per_device(): pl.pallas_call(store_kernel, out_shape=out_shape, in_specs=[vmem, vmem],...  1.05 us

profile of v7, /device:TPU:1, one launch (start us, length us, event | category | flops | bytes accessed | tf_op | source)
XLA Modules:
  0.0 37.5 jit_solution(13559936215608291187)
XLA Ops:
  0.6 35.8 %shard_map.86 = (f32[1,128,2048]{2,1,0:T(8,128)S(1)}, f32[1,128,256]{2,1,0:T(8,128)S(1)}) custom-call(f32[1,128,2048]{2,1,0:T(8,128)} %coef_hbm.1, f32[1,128,2048]{2,1,0:T(8,128)} %sums_hbm.1, bf16[1,2048,4096]{2,1,0:T(8,128)(2,1)} %link_hbm.1, s32[1,8]{1,0:T(1,128)} %starts_hbm.1, s32[1,2048]{1,0:T(1,128)} %ids_hbm.1, f32[1,16]{1,0:T(1,128)} %weight_hbm.1, ...), custom_call_target="tpu_custom_call" | custom-call | tf_op jit(solution)/shard_map/pallas_call | solution.py:657
  36.4 1.0 %shard_map.87 = (f32[1,128,2048]{2,1,0:T(8,128)}, f32[1,128,256]{2,1,0:T(8,128)}) custom-call(f32[1,128,2048]{2,1,0:T(8,128)S(1)} %get-tuple-element.4.updated_in, f32[1,128,256]{2,1,0:T(8,128)S(1)} %get-tuple-element.5.score_in), custom_call_target="tpu_custom_call" | custom-call | tf_op jit(solution)/shard_map/pallas_call | solution.py:695

commit v8 on v7

--- a/solution.py
+++ b/solution.py
@@ -697,7 +697,7 @@
         out_shape=out_shape,
         in_specs=[vmem, vmem],
         out_specs=(hbm, hbm),
-        scratch_shapes=[dma((5,))],
+        scratch_shapes=[dma((2,))],
     )(*(pltpu.with_memory_space_constraint(x, pltpu.VMEM) for x in (updated, scores)))
 
 

time: 37.8 us -> 37.5 us (level)
  no operation moved by 1% of the time
where the time goes in v8:
time: 37.5 us; the launch traced here: 37.1 us
  Pallas kernels  36.5 us (97%)
  between operations  0.64 us (2%)
    pallas_call x1, Pallas kernels, per_device(): pl.pallas_call(functools.partial(step_kernel, sizes), out_shape=out_shape...  35.5 us
    pallas_call x1, Pallas kernels, per_device(): pl.pallas_call(store_kernel, out_shape=out_shape, in_specs=[vmem, vmem],...  1.03 us

profile of v8, /device:TPU:1, one launch (start us, length us, event | category | flops | bytes accessed | tf_op | source)
XLA Modules:
  0.0 37.1 jit_solution(5694391332428962715)
XLA Ops:
  0.6 35.5 %shard_map.86 = (f32[1,128,2048]{2,1,0:T(8,128)S(1)}, f32[1,128,256]{2,1,0:T(8,128)S(1)}) custom-call(f32[1,128,2048]{2,1,0:T(8,128)} %coef_hbm.1, f32[1,128,2048]{2,1,0:T(8,128)} %sums_hbm.1, bf16[1,2048,4096]{2,1,0:T(8,128)(2,1)} %link_hbm.1, s32[1,8]{1,0:T(1,128)} %starts_hbm.1, s32[1,2048]{1,0:T(1,128)} %ids_hbm.1, f32[1,16]{1,0:T(1,128)} %weight_hbm.1, ...), custom_call_target="tpu_custom_call" | custom-call | tf_op jit(solution)/shard_map/pallas_call | solution.py:657
  36.1 1.0 %shard_map.87 = (f32[1,128,2048]{2,1,0:T(8,128)}, f32[1,128,256]{2,1,0:T(8,128)}) custom-call(f32[1,128,2048]{2,1,0:T(8,128)S(1)} %get-tuple-element.4.updated_in, f32[1,128,256]{2,1,0:T(8,128)S(1)} %get-tuple-element.5.score_in), custom_call_target="tpu_custom_call" | custom-call | tf_op jit(solution)/shard_map/pallas_call | solution.py:695
